TPU v7x, 256 devices: a whole 4x4x8 slice. The times are simulated.
256 devices in a mesh: space: 32 (over z, x_hi, core), bead: 8 (over y, x_lo).
Axes of the slice: x: 4 (x_hi: 2, x_lo: 2; x = x_hi * 2 + x_lo), y: 4, z: 8, core: 2. Of those that a mesh axis runs over, the one named last changes fastest.
Arguments:
- positions: float32 [32, 3, 131072], P('bead', None, 'space'), may hold values from -5 to 5
- momenta: float32 [32, 3, 131072], P('bead', None, 'space'), may hold values from -12 to 12
- masses: float32 [131072], P('space'), may hold values from 1 to 16
- strengths: float32 [131072], P('space'), may hold values from 0.5 to 2
- bond_ends: int32 [2, 131072], P(None, 'space'), may hold values from 0 to 127
- angle_ends: int32 [3, 65536], P(None, 'space'), may hold values from 0 to 127
- neighbour_tiles: int32 [3, 1024], P(None, 'space'), may hold values from 0 to 1023, as said below
Outputs:
- new_positions: float32 [32, 3, 131072], P('bead', None, 'space')
- new_momenta: float32 [32, 3, 131072], P('bead', None, 'space')
Inputs may be any that keep to these rules, and one draw needn't show every extreme that they name: `bond_ends`: entry [e, b] is the place within tile b // 128 of end e of bond b. `angle_ends`: entry [e, b] is the place within tile b // 64 of atom e of angle b. `neighbour_tiles`: column t names 3 different tiles, each within 2 tiles of t, counting around the ends (tile 1024 - 1 lies next to tile 0).
All inputs are finite; a program needn't handle non-finite values.
Results may differ from a plain program's by a relative error of at most 0.0003.
Values sent between devices are 32-bit elements; how exact they have to be, the bound alone decides.
A program may use at most 64 MiB of HBM per device.

v0:
```python
import math

import jax
import jax.numpy as jnp
import numpy as np
from jax import lax
from jax.sharding import PartitionSpec as P

BEADS = 32
KEPT = 4
SUBS = 3
TILE = 128
GT = 2
BPT = 128
APT = 64


time_step = 0.3
spring_freq = 80.0
bond_stiff = 0.2
bond_rest = 1.0
angle_stiff = 0.1
angle_rest = 0.5
range_sq = 4.0
HIGH = lax.Precision.HIGHEST


def cut_along(array, dim, length):
    before, after = (array.shape[:dim], array.shape[dim + 1 :])
    return jnp.moveaxis(array.reshape(*before, length, -1, *after), dim, 0)


def edges_of(length, count):
    unit = 8 if length >= 8 * count else 1
    return [length // unit * k // count * unit for k in range(1, count)]


def in_order(parts, dim):
    parts = jnp.moveaxis(parts, 0, dim)
    dims = parts.shape
    return parts.reshape(*dims[:dim], dims[dim] * dims[dim + 1], *dims[dim + 2 :])


def several_exchanges(array, axis, pieces, split_dim, concat_dim):
    parts = cut_along(array, split_dim, lax.axis_size(axis))
    split_at = max(range(1, max(2, parts.ndim - 1)), key=lambda d: parts.shape[d])
    finished = []
    for section in jnp.split(parts, edges_of(parts.shape[split_at], pieces), axis=split_at):
        if section.size:
            finished.append(lax.all_to_all(section, axis, split_axis=0, concat_axis=0, tiled=True))
    return in_order(jnp.concatenate(finished, axis=split_at), concat_dim)


def padded(array, sides, width):
    edges = {}
    for axis, dim in sides:
        size, length = (lax.axis_size(axis), array.shape[dim])
        up = [(i, (i + 1) % size) for i in range(size)]
        last = lax.slice_in_dim(array, length - width, length, axis=dim)
        leading = lax.slice_in_dim(array, 0, width, axis=dim)
        edges[dim] = (
            lax.ppermute(last, axis, up),
            lax.ppermute(leading, axis, [(b, a) for a, b in up]),
        )
    done = []
    for _, dim in sides:
        low, high = edges[dim]
        around = [(width, width) if d in done else (0, 0) for d in range(array.ndim)]
        array = jnp.concatenate([jnp.pad(low, around), array, jnp.pad(high, around)], axis=dim)
        done.append(dim)
    return array


def mode_table(number):
    within = np.arange(number)
    result = np.zeros((number, number))
    for column in range(number):
        if column == 0:
            result[:, column] = 1.0 / math.sqrt(number)
        elif 2 * column < number:
            result[:, column] = math.sqrt(2.0 / number) * np.cos(
                2 * np.pi * within * column / number
            )
        elif 2 * column == number:
            result[:, column] = (-1.0) ** within / math.sqrt(number)
        else:
            result[:, column] = math.sqrt(2.0 / number) * np.sin(
                2 * np.pi * within * column / number
            )
    return result


def contract_table(number, kept):
    larger = mode_table(number)
    smaller = mode_table(kept)
    chosen = [column if 2 * column <= kept else number - kept + column for column in range(kept)]
    return math.sqrt(kept / number) * smaller @ larger[:, chosen].T


def orbit_tables(number, interval):
    freqs = 2.0 * spring_freq * np.sin(np.pi * np.arange(number) / number)
    cosine = np.cos(freqs * interval)
    safe = np.where(freqs > 0, freqs, 1.0)
    gains = np.where(freqs > 0, np.sin(freqs * interval) / safe, interval)
    drags = freqs * np.sin(freqs * interval)
    return (cosine, gains, drags)


def propagate(current, moment, masses, modes_table, cosine, gains, drags):
    modes_pos = jnp.einsum("jk,jcl->kcl", modes_table, current, precision=HIGH)
    modes_mom = jnp.einsum("jk,jcl->kcl", modes_table, moment, precision=HIGH)
    moved_pos = cosine[:, None, None] * modes_pos + gains[:, None, None] * modes_mom / masses
    moved_mom = cosine[:, None, None] * modes_mom - drags[:, None, None] * masses * modes_pos
    return (
        jnp.einsum("jk,kcl->jcl", modes_table, moved_pos, precision=HIGH),
        jnp.einsum("jk,kcl->jcl", modes_table, moved_mom, precision=HIGH),
    )


def pair_block(own_tiles, nearby, own_scale, nearby_scale):
    own_sq = jnp.sum(own_tiles * own_tiles, axis=1)
    nearby_sq = jnp.sum(nearby * nearby, axis=1)
    inner = jnp.einsum("cxta,cxtn->ctan", own_tiles, nearby, precision=HIGH)
    distance = own_sq[..., None] + nearby_sq[:, :, None, :] - 2.0 * inner
    weight = jnp.exp(-distance / range_sq) * nearby_scale[None, :, None, :]
    weight_sum = jnp.sum(weight, axis=3)
    pulled = jnp.einsum("ctan,cxtn->cxta", weight, nearby, precision=HIGH)
    return 2.0 / range_sq * own_scale[None, None] * (own_tiles * weight_sum[:, None] - pulled)


def tile_forces(extended, scale_ext, own_first, tile_count, local_nbr):
    kept = extended.shape[0]
    tiled = extended.reshape(kept, 3, -1, TILE)
    scale_tiles = scale_ext.reshape(-1, TILE)
    group_size = math.gcd(tile_count, 8)
    rounds = tile_count // group_size
    width = local_nbr.shape[1]

    def one_group(offset):
        own_tiles = lax.dynamic_slice_in_dim(tiled, own_first + offset, group_size, 2)
        own_scale = lax.dynamic_slice_in_dim(scale_tiles, own_first + offset, group_size, 0)
        chosen = local_nbr.reshape(-1)
        nearby = jnp.take(tiled, chosen, axis=2).reshape(kept, 3, group_size, width * TILE)
        nearby_scale = jnp.take(scale_tiles, chosen, axis=0).reshape(group_size, width * TILE)
        return pair_block(own_tiles, nearby, own_scale, nearby_scale)

    offsets = jnp.arange(rounds, dtype=jnp.int32) * group_size
    result = lax.map(one_group, offsets)
    return jnp.moveaxis(result, 0, 2).reshape(kept, 3, tile_count * TILE)


def build_tables(bond_ends, angle_ends):
    places = lax.broadcasted_iota(jnp.int32, (1, 1, 1, TILE), 3)
    bond_tiles = bond_ends.reshape(2, -1, BPT)
    angle_tiles = angle_ends.reshape(3, -1, APT)
    bond_hot = (bond_tiles[..., None] == places).astype(jnp.float32)
    angle_hot = (angle_tiles[..., None] == places).astype(jnp.float32)
    return (bond_hot, angle_hot)


def bonded(current, hot_tables):
    bond_hot, angle_hot = hot_tables
    bead_total = current.shape[0]
    length = current.shape[2]
    tiled = current.reshape(bead_total, 3, length // TILE, TILE)

    def select(one_hot):
        return jnp.einsum("bcta,tga->bctg", tiled, one_hot, precision=HIGH)

    def deposit(values_in, one_hot):
        return jnp.einsum("bctg,tga->bcta", values_in, one_hot, precision=HIGH)

    stretch = select(bond_hot[0]) - select(bond_hot[1])
    factor = bond_stiff * (jnp.sum(stretch * stretch, axis=1, keepdims=True) - bond_rest)
    push = -factor * stretch
    forces = deposit(push, bond_hot[0]) - deposit(push, bond_hot[1])
    centre = select(angle_hot[1])
    to_first = select(angle_hot[0]) - centre
    to_last = select(angle_hot[2]) - centre
    factor = angle_stiff * (jnp.sum(to_first * to_last, axis=1, keepdims=True) - angle_rest)
    forces = forces + deposit(-factor * to_last, angle_hot[0])
    forces = forces + deposit(-factor * to_first, angle_hot[2])
    forces = forces + deposit(factor * (to_first + to_last), angle_hot[1])
    return forces.reshape(bead_total, 3, length)


def kick_drift(current, moment, nonbonded, hot_tables, advance):
    interval = time_step / SUBS
    moment = moment + 0.5 * time_step * nonbonded(current)
    pushed = bonded(current, hot_tables)
    for substep in range(SUBS):
        moment = moment + 0.5 * interval * pushed
        current, moment = advance(current, moment)
        pushed = bonded(current, hot_tables)
        moment = moment + 0.5 * interval * pushed
    moment = moment + 0.5 * time_step * nonbonded(current)
    return (current, moment)


def body(positions, momenta, masses, strengths, bond_ends, angle_ends, neighbour_tiles):
    slab = positions.shape[2]
    bead_count = lax.axis_size("bead")
    bead_index = lax.axis_index("bead")
    space_count = lax.axis_size("space")
    space_index = lax.axis_index("space")
    block_atoms = slab // bead_count
    slab_tiles = slab // TILE
    block_tiles = block_atoms // TILE
    all_tiles = slab_tiles * space_count
    rim_width = GT * TILE
    interval = time_step / SUBS
    modes_table = jnp.asarray(mode_table(BEADS), jnp.float32)
    contract = jnp.asarray(contract_table(BEADS, KEPT), jnp.float32)
    expand = BEADS / KEPT * contract.T
    cos_np, gain_np, drag_np = orbit_tables(BEADS, interval)
    cosine = jnp.asarray(cos_np, jnp.float32)
    gains = jnp.asarray(gain_np, jnp.float32)
    drags = jnp.asarray(drag_np, jnp.float32)
    my_nbr = lax.dynamic_slice_in_dim(neighbour_tiles, bead_index * block_tiles, block_tiles, 1)
    my_masses = lax.dynamic_slice_in_dim(masses, bead_index * block_atoms, block_atoms, 0)

    def nearby_forces(packed_ext, own_first, local_nbr):
        extended = packed_ext[: KEPT * 3].reshape(KEPT, 3, -1)
        return tile_forces(extended, packed_ext[KEPT * 3], own_first, block_tiles, local_nbr)

    current, moment = (
        several_exchanges(positions, "bead", 2, 2, 0),
        several_exchanges(momenta, "bead", 2, 2, 0),
    )
    my_bonds = lax.dynamic_slice_in_dim(
        bond_ends, bead_index * block_tiles * BPT, block_tiles * BPT, 1
    )
    my_angles = lax.dynamic_slice_in_dim(
        angle_ends, bead_index * block_tiles * APT, block_tiles * APT, 1
    )
    hot_tables = build_tables(my_bonds, my_angles)
    my_strengths = lax.dynamic_slice_in_dim(strengths, bead_index * block_atoms, block_atoms, 0)
    local_nbr = jnp.mod(
        my_nbr - ((space_index * bead_count + bead_index) * block_tiles - GT), all_tiles
    ).T

    def nonbonded(current):
        contracted = jnp.einsum("kj,jcl->kcl", contract, current, precision=HIGH)
        packed = jnp.concatenate(
            [contracted.reshape(KEPT * 3, block_atoms), my_strengths[None, :]], 0
        )
        extended = padded(packed, ((("space", "bead"), 1),), rim_width)
        nearby = nearby_forces(extended, GT, local_nbr)
        return jnp.einsum("jk,kcl->jcl", expand, nearby, precision=HIGH)

    def advance(current, moment):
        return propagate(current, moment, my_masses, modes_table, cosine, gains, drags)

    current, moment = kick_drift(current, moment, nonbonded, hot_tables, advance)
    return (
        lax.all_to_all(current, "bead", split_axis=0, concat_axis=2, tiled=True),
        lax.all_to_all(moment, "bead", split_axis=0, concat_axis=2, tiled=True),
    )


def solution(mesh):
    placed = (
        P("bead", None, "space"),
        P("bead", None, "space"),
        P("space"),
        P("space"),
        P(None, "space"),
        P(None, "space"),
        P(None, "space"),
    )
    return jax.shard_map(
        body,
        mesh=mesh,
        in_specs=placed,
        out_specs=(P("bead", None, "space"), P("bead", None, "space")),
        check_vma=False,
    )
```

profile of v0, /device:TPU:8, one launch (start us, length us, event | category | flops | bytes accessed | tf_op | source)
XLA Modules:
  0.0 110.1 jit_solution(17677359356519072048)
XLA Ops:
  0.6 1.1 reshape.197
  1.7 0.7 copy.231
  2.5 5.8 %all-to-all-start = ((f32[8,2,3,512]{3,1,2,0:T(2,128)}), f32[8,2,3,512]{3,1,2,0:T(2,128)S(1)}, u32[]{:S(2)}, u32[]{:S(2)}) async-start(f32[8,2,3,512]{3,1,2,0:T(2,128)} %copy.231), calls=%async_computation | async-start | bytes 196608 | tf_op jit(solution)/shard_map/all_to_all | solution.py:50
  8.3 0.8 fusion.168
  9.5 0.7 copy.232
  10.2 0.7 constant_dynamic-slice_fusion
  11.2 1.1 reshape.199
  12.3 0.7 copy.234
  13.0 0.7 copy.235
  13.7 0.8 dynamic_slice.37
  14.5 0.7 broadcast_multiply_fusion
  15.2 5.7 %all-to-all-start.1 = ((f32[8,2,3,512]{3,1,2,0:T(2,128)}), f32[8,2,3,512]{3,1,2,0:T(2,128)S(1)}, u32[]{:S(2)}, u32[]{:S(2)}) async-start(f32[8,2,3,512]{3,1,2,0:T(2,128)} %copy.232), calls=%async_computation.1 | async-start | bytes 196608 | tf_op jit(solution)/shard_map/all_to_all | solution.py:50
  20.9 0.8 multiply_bitcast_fusion
  21.7 4.2 %all-to-all-done.1 = f32[8,2,3,512]{3,1,2,0:T(2,128)S(1)} async-done(((f32[8,2,3,512]{3,1,2,0:T(2,128)}), f32[8,2,3,512]{3,1,2,0:T(2,128)S(1)}, u32[]{:S(2)}, u32[]{:S(2)}) %all-to-all-start.1) | async-done | bytes 98336 | tf_op jit(solution)/shard_map/all_to_all | solution.py:50
  25.9 4.8 %all-to-all-start.2 = ((f32[8,2,3,512]{3,1,2,0:T(2,128)}), f32[8,2,3,512]{3,1,2,0:T(2,128)S(1)}, u32[]{:S(2)}, u32[]{:S(2)}) async-start(f32[8,2,3,512]{3,1,2,0:T(2,128)} %copy.234), calls=%async_computation.2 | async-start | bytes 196608 | tf_op jit(solution)/shard_map/all_to_all | solution.py:50
  31.4 0.4 multiply_reduce_fusion.7
  33.5 1.6 %collective-permute-start = (f32[13,256]{1,0:T(8,128)S(1)}, f32[13,256]{1,0:T(8,128)S(1)}, u32[]{:S(2)}, u32[]{:S(2)}) collective-permute-start(f32[13,256]{1,0:T(8,128)S(1)} %get-tuple-element.54), channel_id=1, source_target_pairs={{0,1},{1,2},{2,3},{3,4},{4,5},{5,6},{6,7},{7,8},{8,9},{9,10},{10,1... | collective-permute-start | bytes 39944 | tf_op jit(solution)/shard_map/ppermute | solution.py:62
  35.1 1.5 %collective-permute-start.1 = (f32[13,256]{1,0:T(8,128)S(1)}, f32[13,256]{1,0:T(8,128)S(1)}, u32[]{:S(2)}, u32[]{:S(2)}) collective-permute-start(f32[13,256]{1,0:T(8,128)S(1)} %get-tuple-element.55), channel_id=1, source_target_pairs={{1,0},{2,1},{3,2},{4,3},{5,4},{6,5},{7,6},{8,7},{9,8},{10,9},{11,1... | collective-permute-start | bytes 39944 | tf_op jit(solution)/shard_map/ppermute | solution.py:63
  37.3 8.3 %all-to-all-start.3 = ((f32[8,2,3,512]{3,1,2,0:T(2,128)}), f32[8,2,3,512]{3,1,2,0:T(2,128)S(1)}, u32[]{:S(2)}, u32[]{:S(2)}) async-start(f32[8,2,3,512]{3,1,2,0:T(2,128)} %copy.235), calls=%async_computation.3 | async-start | bytes 196608 | tf_op jit(solution)/shard_map/all_to_all | solution.py:50
  45.9 4.8 %all-to-all-done.3 = f32[8,2,3,512]{3,1,2,0:T(2,128)S(1)} async-done(((f32[8,2,3,512]{3,1,2,0:T(2,128)}), f32[8,2,3,512]{3,1,2,0:T(2,128)S(1)}, u32[]{:S(2)}, u32[]{:S(2)}) %all-to-all-start.3) | async-done | bytes 98336 | tf_op jit(solution)/shard_map/all_to_all | solution.py:50
  51.0 0.6 gather_fusion
  51.8 0.6 gather_fusion.1
  52.5 4.5 %fusion.175 = (f32[4,4,128]{2,1,0:T(4,128)S(1)}, f32[4,4,128,384]{3,2,1,0:T(8,128)S(1)}) fusion(f32[4,384]{1,0:T(4,128)S(1)} %mul.528, f32[4,3,4,384]{3,2,1,0:T(4,128)S(1)} %reshape.203, f32[4,3,4,128]{3,2,1,0:T(4,128)S(1)} %dynamic_slice.39, f32[4,4,384]{2,1,0:T(4,128)S(1)} %add.255, f32[4,4,128]{2,1,0:T(4,128)S(1)} %fusion.163), kind=kOutput, calls=%fused_computation.274 | convolution fusion | flops 33814528 | bytes 3291136 | tf_op jit(solution)/shard_map/while/body/eval_jaxpr/cxta,cxtn->ctan/dot_general | solution.py:123
  57.0 3.5 %fusion.27 = f32[4,3,4,128]{3,1,2,0:T(4,128)S(1)} fusion(f32[4,4,128,384]{3,2,1,0:T(8,128)S(1)} %get-tuple-element.57, f32[4,3,4,384]{3,2,1,0:T(4,128)S(1)} %reshape.203, f32[4,3,4,128]{3,2,1,0:T(4,128)S(1)} %dynamic_slice.39, f32[4,4,128]{2,1,0:T(4,128)S(1)} %get-tuple-element.56, f32[4,128]{1,0:T(4,128)S(1)} %get-tuple-element.31), kind=kOutput, calls=%fused_computation.68 | convolution fusion | flops 28329984 | bytes 3278848 | tf_op jit(solution)/shard_map/while/body/eval_jaxpr/ctan,cxtn->cxta/dot_general | solution.py:127
  60.6 0.4 fusion.24
  61.3 0.4 fusion.52
  63.2 0.4 multiply_reduce_fusion.5
  64.9 0.4 fusion.17
  65.6 0.4 fusion.51
  67.0 0.4 fusion.8
  67.7 0.4 multiply_reduce_fusion.3
  69.4 0.4 fusion.11
  70.1 0.4 fusion.50
  71.3 0.8 copy.270
  72.7 0.4 multiply_reduce_fusion.1
  73.7 0.9 collective-permute-start.2
  74.7 2.1 %collective-permute-start.3 = (f32[13,256]{1,0:T(8,128)S(1)}, f32[13,256]{1,0:T(8,128)S(1)}, u32[]{:S(2)}, u32[]{:S(2)}) collective-permute-start(f32[13,256]{1,0:T(8,128)S(1)} %get-tuple-element.53), channel_id=1, source_target_pairs={{1,0},{2,1},{3,2},{4,3},{5,4},{6,5},{7,6},{8,7},{9,8},{10,9},{11,1... | collective-permute-start | bytes 39944 | tf_op jit(solution)/shard_map/ppermute | solution.py:63
  76.8 9.1 %all-to-all-start.4 = ((f32[32,3,512]{2,1,0:T(4,128)}), f32[32,3,512]{2,1,0:T(4,128)S(1)}, u32[]{:S(2)}, u32[]{:S(2)}) async-start(f32[32,3,512]{2,1,0:T(4,128)} %copy.270), calls=%async_computation.4 | async-start | bytes 524288 | tf_op jit(solution)/shard_map/all_to_all | solution.py:256
  86.8 0.6 gather_fusion.2
  87.6 0.6 gather_fusion.3
  88.3 4.5 %fusion.176 = (f32[4,4,128]{2,1,0:T(4,128)S(1)}, f32[4,4,128,384]{3,2,1,0:T(8,128)S(1)}) fusion(f32[4,384]{1,0:T(4,128)S(1)} %mul.610, f32[4,3,4,384]{3,2,1,0:T(4,128)S(1)} %reshape.208, f32[4,3,4,128]{3,2,1,0:T(4,128)S(1)} %dynamic_slice.40, f32[4,4,384]{2,1,0:T(4,128)S(1)} %add.290, f32[4,4,128]{2,1,0:T(4,128)S(1)} %fusion.164), kind=kOutput, calls=%fused_computation.275 | convolution fusion | flops 33814528 | bytes 3291136 | tf_op jit(solution)/shard_map/while/body/eval_jaxpr/cxta,cxtn->ctan/dot_general | solution.py:123
  92.8 3.5 %fusion.28 = f32[4,3,4,128]{3,1,2,0:T(4,128)S(1)} fusion(f32[4,4,128,384]{3,2,1,0:T(8,128)S(1)} %get-tuple-element.71, f32[4,3,4,384]{3,2,1,0:T(4,128)S(1)} %reshape.208, f32[4,3,4,128]{3,2,1,0:T(4,128)S(1)} %dynamic_slice.40, f32[4,4,128]{2,1,0:T(4,128)S(1)} %get-tuple-element.70, f32[4,128]{1,0:T(4,128)S(1)} %get-tuple-element.31), kind=kOutput, calls=%fused_computation.69 | convolution fusion | flops 28329984 | bytes 3278848 | tf_op jit(solution)/shard_map/while/body/eval_jaxpr/ctan,cxtn->cxta/dot_general | solution.py:127
  96.3 0.4 convolution_multiply_fusion
  97.1 0.8 copy.287
  97.9 5.7 %all-to-all-start.5 = ((f32[32,3,512]{2,1,0:T(4,128)}), f32[32,3,512]{2,1,0:T(4,128)S(1)}, u32[]{:S(2)}, u32[]{:S(2)}) async-start(f32[32,3,512]{2,1,0:T(4,128)} %copy.287), calls=%async_computation.5 | async-start | bytes 524288 | tf_op jit(solution)/shard_map/all_to_all | solution.py:257
  103.8 0.8 all_to_all.45
  104.6 4.6 %all-to-all-done.5 = f32[32,3,512]{2,1,0:T(4,128)S(1)} async-done(((f32[32,3,512]{2,1,0:T(4,128)}), f32[32,3,512]{2,1,0:T(4,128)S(1)}, u32[]{:S(2)}, u32[]{:S(2)}) %all-to-all-start.5) | async-done | bytes 196640 | tf_op jit(solution)/shard_map/all_to_all | solution.py:257
  109.3 0.8 all_to_all.49
  (130 shorter events, 14.4 us)
Async XLA Ops:
  0.6 8.6 %copy-start = (s32[2,4096]{1,0:T(2,128)S(1)}, s32[2,4096]{1,0:T(2,128)}, u32[]{:S(2)}) copy-start(s32[2,4096]{1,0:T(2,128)} %param.20) | copy-start | bytes 98308
  2.5 12.7 %all-to-all-start = ((f32[8,2,3,512]{3,1,2,0:T(2,128)}), f32[8,2,3,512]{3,1,2,0:T(2,128)S(1)}, u32[]{:S(2)}, u32[]{:S(2)}) async-start(f32[8,2,3,512]{3,1,2,0:T(2,128)} %copy.231), calls=%async_computation | async-start | bytes 196608 | tf_op jit(solution)/shard_map/all_to_all | solution.py:50
  15.2 10.7 %all-to-all-start.1 = ((f32[8,2,3,512]{3,1,2,0:T(2,128)}), f32[8,2,3,512]{3,1,2,0:T(2,128)S(1)}, u32[]{:S(2)}, u32[]{:S(2)}) async-start(f32[8,2,3,512]{3,1,2,0:T(2,128)} %copy.232), calls=%async_computation.1 | async-start | bytes 196608 | tf_op jit(solution)/shard_map/all_to_all | solution.py:50
  25.9 11.4 %all-to-all-start.2 = ((f32[8,2,3,512]{3,1,2,0:T(2,128)}), f32[8,2,3,512]{3,1,2,0:T(2,128)S(1)}, u32[]{:S(2)}, u32[]{:S(2)}) async-start(f32[8,2,3,512]{3,1,2,0:T(2,128)} %copy.234), calls=%async_computation.2 | async-start | bytes 196608 | tf_op jit(solution)/shard_map/all_to_all | solution.py:50
  30.7 2.5 %copy-start.3 = (f32[4,32,1]{1,0,2:T(4,128)S(1)}, f32[4,32,1]{1,0,2:T(4,128)}, u32[]{:S(2)}) copy-start(f32[4,32,1]{1,0,2:T(4,128)} %constant.162) | copy-start | bytes 1540
  31.0 6.0 %copy-start.1 = (f32[32,32,1]{0,1,2:T(8,128)S(1)}, f32[32,32,1]{0,1,2:T(8,128)}, u32[]{:S(2)}) copy-start(f32[32,32,1]{0,1,2:T(8,128)} %constant.160) | copy-start | bytes 12292
  33.5 17.4 %collective-permute-start = (f32[13,256]{1,0:T(8,128)S(1)}, f32[13,256]{1,0:T(8,128)S(1)}, u32[]{:S(2)}, u32[]{:S(2)}) collective-permute-start(f32[13,256]{1,0:T(8,128)S(1)} %get-tuple-element.54), channel_id=1, source_target_pairs={{0,1},{1,2},{2,3},{3,4},{4,5},{5,6},{6,7},{7,8},{8,9},{9,10},{10,1... | collective-permute-start | bytes 39944 | tf_op jit(solution)/shard_map/ppermute | solution.py:62
  35.1 15.8 %collective-permute-start.1 = (f32[13,256]{1,0:T(8,128)S(1)}, f32[13,256]{1,0:T(8,128)S(1)}, u32[]{:S(2)}, u32[]{:S(2)}) collective-permute-start(f32[13,256]{1,0:T(8,128)S(1)} %get-tuple-element.55), channel_id=1, source_target_pairs={{1,0},{2,1},{3,2},{4,3},{5,4},{6,5},{7,6},{8,7},{9,8},{10,9},{11,1... | collective-permute-start | bytes 39944 | tf_op jit(solution)/shard_map/ppermute | solution.py:63
  37.3 13.4 %all-to-all-start.3 = ((f32[8,2,3,512]{3,1,2,0:T(2,128)}), f32[8,2,3,512]{3,1,2,0:T(2,128)S(1)}, u32[]{:S(2)}, u32[]{:S(2)}) async-start(f32[8,2,3,512]{3,1,2,0:T(2,128)} %copy.235), calls=%async_computation.3 | async-start | bytes 196608 | tf_op jit(solution)/shard_map/all_to_all | solution.py:50
  57.0 3.5 %copy-start.2 = (f32[4,32,1]{1,0,2:T(4,128)S(1)}, f32[4,32,1]{1,0,2:T(4,128)}, u32[]{:S(2)}) copy-start(f32[4,32,1]{1,0,2:T(4,128)} %constant.161) | copy-start | bytes 1540
  57.0 4.3 %copy-start.4 = (f32[32]{0:T(128)S(1)}, f32[32]{0:T(128)}, u32[]{:S(2)}) copy-start(f32[32]{0:T(128)} %constant.154.clone) | copy-start | bytes 388
  57.0 4.2 %copy-start.5 = (f32[32]{0:T(128)S(1)}, f32[32]{0:T(128)}, u32[]{:S(2)}) copy-start(f32[32]{0:T(128)} %constant.155.clone) | copy-start | bytes 388
  73.7 12.9 %collective-permute-start.2 = (f32[13,256]{1,0:T(8,128)S(1)}, f32[13,256]{1,0:T(8,128)S(1)}, u32[]{:S(2)}, u32[]{:S(2)}) collective-permute-start(f32[13,256]{1,0:T(8,128)S(1)} %get-tuple-element.52), channel_id=1, source_target_pairs={{0,1},{1,2},{2,3},{3,4},{4,5},{5,6},{6,7},{7,8},{8,9},{9,10},{10,1... | collective-permute-start | bytes 39944 | tf_op jit(solution)/shard_map/ppermute | solution.py:62
  74.7 12.0 %collective-permute-start.3 = (f32[13,256]{1,0:T(8,128)S(1)}, f32[13,256]{1,0:T(8,128)S(1)}, u32[]{:S(2)}, u32[]{:S(2)}) collective-permute-start(f32[13,256]{1,0:T(8,128)S(1)} %get-tuple-element.53), channel_id=1, source_target_pairs={{1,0},{2,1},{3,2},{4,3},{5,4},{6,5},{7,6},{8,7},{9,8},{10,9},{11,1... | collective-permute-start | bytes 39944 | tf_op jit(solution)/shard_map/ppermute | solution.py:63
  76.8 21.1 %all-to-all-start.4 = ((f32[32,3,512]{2,1,0:T(4,128)}), f32[32,3,512]{2,1,0:T(4,128)S(1)}, u32[]{:S(2)}, u32[]{:S(2)}) async-start(f32[32,3,512]{2,1,0:T(4,128)} %copy.270), calls=%async_computation.4 | async-start | bytes 524288 | tf_op jit(solution)/shard_map/all_to_all | solution.py:256
  97.9 11.2 %all-to-all-start.5 = ((f32[32,3,512]{2,1,0:T(4,128)}), f32[32,3,512]{2,1,0:T(4,128)S(1)}, u32[]{:S(2)}, u32[]{:S(2)}) async-start(f32[32,3,512]{2,1,0:T(4,128)} %copy.287), calls=%async_computation.5 | async-start | bytes 524288 | tf_op jit(solution)/shard_map/all_to_all | solution.py:257
where the time goes:
time: 112 us; the launch traced here: 110 us
  starting transfers between devices  45.6 us (41%)
  matrix products  32.6 us (29%)
  waiting for transfers between devices  13.6 us (12%)
  local copies, waits for them, and re-layouts  13.3 us (12%)
  other arithmetic  3.39 us (3%)
  between operations  1.61 us (1%)
    all_to_all x4, starting transfers between devices, several_exchanges(): lax.all_to_all(section, axis, split_axis=0, concat_axis=0, tiled=True)  24.7 us
    all_to_all x1, starting transfers between devices, body(): lax.all_to_all(current, 'bead', split_axis=0, concat_axis=2, tiled=True)  9.15 us
    dot_general x2, matrix products, pair_block(): inner = jnp.einsum('cxta,cxtn->ctan', own_tiles, nearby, precision=HIGH)  9.02 us
    all_to_all x4, waiting for transfers between devices, several_exchanges(): lax.all_to_all(section, axis, split_axis=0, concat_axis=0, tiled=True)  8.98 us
    dot_general x2, matrix products, pair_block(): pulled = jnp.einsum('ctan,cxtn->cxta', weight, nearby, precision=HIGH)  6.91 us
    dot_general x20, matrix products, select(): return jnp.einsum('bcta,tga->bctg', tiled, one_hot, precision=HIGH)  6.36 us
    all_to_all x1, starting transfers between devices, body(): lax.all_to_all(moment, 'bead', split_axis=0, concat_axis=2, tiled=True)  5.73 us
    dot_general x20, matrix products, deposit(): return jnp.einsum('bctg,tga->bcta', values_in, one_hot, precision=HIGH)  4.95 us
  transfers between devices with their start and end apart: 10, of which 3 were waited for; matrix products, arithmetic and copies ran while one was open for 21% of the time, Pallas kernels for 0%

commit v1 on v0

v1 whole, which is shorter than its diff:
```python
import functools
import math

import jax
import jax.numpy as jnp
import ml_dtypes
import numpy as np
from jax import lax
from jax.experimental import pallas as pl
from jax.experimental.pallas import tpu as pltpu
from jax.sharding import PartitionSpec as P

BEADS = 32
KEPT = 4
SUBS = 3
TILE = 128
GT = 2
NBR = 3
BPT = 128
APT = 64

time_step = 0.3
spring_freq = 80.0
bond_stiff = 0.2
bond_rest = 1.0
angle_stiff = 0.1
angle_rest = 0.5
range_sq = 4.0

F32 = jnp.float32
BF16 = jnp.bfloat16
MESH = pl.DeviceIdType.MESH


def mode_table(number):
    within = np.arange(number)
    result = np.zeros((number, number))
    for column in range(number):
        if column == 0:
            result[:, column] = 1.0 / math.sqrt(number)
        elif 2 * column < number:
            result[:, column] = math.sqrt(2.0 / number) * np.cos(2 * np.pi * within * column / number)
        elif 2 * column == number:
            result[:, column] = (-1.0) ** within / math.sqrt(number)
        else:
            result[:, column] = math.sqrt(2.0 / number) * np.sin(2 * np.pi * within * column / number)
    return result


def contract_table(number, kept):
    larger = mode_table(number)
    smaller = mode_table(kept)
    chosen = [column if 2 * column <= kept else number - kept + column for column in range(kept)]
    return math.sqrt(kept / number) * smaller @ larger[:, chosen].T


def halves(table):
    high = table.astype(ml_dtypes.bfloat16)
    low = (table - high.astype(np.float64)).astype(ml_dtypes.bfloat16)
    return high, low


def three_products(table):
    high, low = halves(table)
    return np.concatenate([high, low, high], axis=1)


def constant_table():
    modes = mode_table(BEADS)
    interval = time_step / SUBS
    freqs = 2.0 * spring_freq * np.sin(np.pi * np.arange(BEADS) / BEADS)
    safe = np.where(freqs > 0, freqs, 1.0)
    cosine = np.cos(freqs * interval)
    gains = np.where(freqs > 0, np.sin(freqs * interval) / safe, interval)
    drags = freqs * np.sin(freqs * interval)
    keep = (modes * cosine) @ modes.T
    gain = (modes * gains) @ modes.T
    drag = -(modes * drags) @ modes.T
    free = np.block([[keep, gain], [drag, keep]])
    contract = contract_table(BEADS, KEPT)
    narrow = np.zeros((16, 3 * BEADS))
    for k in range(KEPT):
        for c in range(3):
            narrow[3 * k + c, c * BEADS : (c + 1) * BEADS] = contract[k]
    expand = BEADS / KEPT * contract.T
    wide = np.zeros((3 * BEADS, 16))
    for k in range(KEPT):
        for c in range(3):
            wide[c * BEADS : (c + 1) * BEADS, 3 * k + c] = expand[:, k]
    wide *= 0.5 * time_step * 2.0 / range_sq
    table = np.zeros((64 + 16 + 96, 384), ml_dtypes.bfloat16)
    table[:64, :192] = three_products(free)
    table[64:80, :288] = three_products(narrow)
    table[80:176, :48] = three_products(wide)
    return table


def split2(x):
    high = x.astype(BF16)
    return high, (x - high.astype(F32)).astype(BF16)


def split3(x):
    high = x.astype(BF16)
    rest = x - high.astype(F32)
    middle = rest.astype(BF16)
    return high, middle, (rest - middle.astype(F32)).astype(BF16)


def mm(a, b):
    return jnp.dot(a, b, preferred_element_type=F32)


def lanes(x, t):
    return x[:, t * TILE : (t + 1) * TILE]


def kernel(
    spaces,
    beads,
    q_in,
    p_in,
    mass_in,
    strength_in,
    bond_in,
    angle_in,
    nbr_in,
    const_in,
    q_out,
    p_out,
    q_stage,
    p_stage,
    q_all,
    p_all,
    q_done,
    p_done,
    mass_v,
    strength_v,
    bond_v,
    angle_v,
    nbr_s,
    const_v,
    pick,
    drop,
    ext,
    a_side,
    g_side,
    local_sem,
    send_sem,
    recv_sem,
    own_sem,
    halo_send,
    halo_recv,
):
    space = lax.axis_index("space")
    me = lax.axis_index("bead")
    slab = q_in.shape[2]
    own = slab // beads
    tiles = own // TILE
    held = q_in.shape[1]
    total = spaces * beads
    spot = space * beads + me
    after = lax.rem(spot + 1, total)
    before = lax.rem(spot + total - 1, total)
    after_id = (lax.div(after, beads), lax.rem(after, beads))
    before_id = (lax.div(before, beads), lax.rem(before, beads))
    peers = [lax.rem(me + d, beads) for d in range(1, beads)]
    order = sorted(range(beads - 1), key=lambda n: -min(n + 1, beads - n - 1))

    barrier = pltpu.get_barrier_semaphore()
    for peer in peers:
        pl.semaphore_signal(barrier, inc=1, device_id=(space, peer), device_id_type=MESH)
    for device in (before_id, after_id):
        pl.semaphore_signal(barrier, inc=1, device_id=device, device_id_type=MESH)

    my_rows = pl.ds(pl.multiple_of(held * me, held), held)
    my_lanes = pl.ds(pl.multiple_of(own * me, own), own)
    local = [
        (q_in, q_stage),
        (p_in, p_stage),
        (q_in.at[:, :, my_lanes], q_all.at[:, my_rows, :]),
        (p_in.at[:, :, my_lanes], p_all.at[:, my_rows, :]),
        (bond_in.at[:, my_lanes], bond_v),
        (angle_in.at[:, pl.ds(pl.multiple_of((own // 2) * me, own // 2), own // 2)], angle_v),
        (mass_in, mass_v),
        (strength_in, strength_v),
        (nbr_in, nbr_s),
        (const_in, const_v),
    ]
    local = [pltpu.make_async_copy(a, b, local_sem.at[n]) for n, (a, b) in enumerate(local)]
    for copy in local:
        copy.start()

    def exchange(kind, source, target):
        copies = []
        for n in order:
            peer = peers[n]
            copies.append(
                pltpu.make_async_remote_copy(
                    src_ref=source(peer),
                    dst_ref=target,
                    send_sem=send_sem.at[kind, n],
                    recv_sem=recv_sem.at[kind, n],
                    device_id=(space, peer),
                    device_id_type=MESH,
                )
            )
        for copy in copies:
            copy.start()
        return copies

    def lanes_of(ref):
        return lambda peer: ref.at[:, :, pl.ds(pl.multiple_of(own * peer, own), own)]

    def rows_of(ref):
        return lambda peer: ref.at[:, pl.ds(pl.multiple_of(held * peer, held), held), :]

    pl.semaphore_wait(barrier, beads + 1)
    local[0].wait()
    sends = exchange(0, lanes_of(q_stage), q_all.at[:, my_rows, :])
    q_sends = list(sends)
    local[1].wait()
    p_sends = exchange(1, lanes_of(p_stage), p_all.at[:, my_rows, :])
    sends = sends + p_sends

    for n in (4, 5, 6, 7, 8, 9):
        local[n].wait()

    place = lax.broadcasted_iota(jnp.int32, (TILE, TILE), 0)
    lane = lax.broadcasted_iota(jnp.int32, (8, TILE), 1)

    def hot(row):
        return jnp.where(place == row, 1.0, 0.0).astype(F32)

    for t in range(tiles):
        ends = bond_v[:, t * TILE : (t + 1) * TILE]
        bonds = hot(ends[0:1]) - hot(ends[1:2])
        pair = angle_v[:, (t // 2) * TILE : (t // 2 + 1) * TILE]
        rows = [jnp.broadcast_to(pair[e : e + 1], (8, TILE)) for e in range(3)]
        turned = [pltpu.roll(r, APT, 1) for r in rows]
        left, right = (rows, turned) if t % 2 == 0 else (turned, rows)
        outer = jnp.where(lane < APT, left[0], right[2])[0:1]
        centre = jnp.where(lane < APT, left[1], right[1])[0:1]
        angles = hot(outer) - hot(centre)
        pick[t] = jnp.concatenate([bonds, angles], axis=1).astype(BF16)
        drop[t] = jnp.concatenate([jnp.transpose(bonds), jnp.transpose(angles)], axis=0).astype(BF16)

    mass_row = jnp.concatenate([mass_v[pl.ds(tiles * me + t, 1), :] for t in range(tiles)], axis=1)
    inverse = 1.0 / mass_row
    strengths = [strength_v[pl.ds(tiles * me + t, 1), :] for t in range(tiles)]

    free_table = const_v[0:64, 0:192]
    narrow_table = const_v[64:80, 0:288]
    wide_table = const_v[80:176, 0:48]

    row16 = lax.broadcasted_iota(jnp.int32, (16, TILE), 0)
    feature = row16 < 12

    def contracted(current):
        high, low = split2(jnp.concatenate(current, axis=0))
        return mm(narrow_table, jnp.concatenate([high, high, low], axis=0))

    def start_halo(turn, narrow):
        for t in range(tiles):
            ext[turn, GT + t] = jnp.where(feature, lanes(narrow, t), strengths[t])
        copies = []
        for side, device, source, target in (
            (0, before_id, GT, GT + tiles),
            (1, after_id, tiles, 0),
        ):
            copies.append(
                pltpu.make_async_remote_copy(
                    src_ref=ext.at[turn, pl.ds(source, GT)],
                    dst_ref=ext.at[turn, pl.ds(target, GT)],
                    send_sem=halo_send.at[turn, side],
                    recv_sem=halo_recv.at[turn, side],
                    device_id=device,
                    device_id_type=MESH,
                )
            )
        for copy in copies:
            copy.start()
        return copies

    scale = math.sqrt(2.0 / range_sq * math.log2(math.e))

    def sides(turn, u, with_own):
        block = ext[turn, u]
        scaled = block * scale
        square = scaled * scaled
        norms = scaled
        for k in range(KEPT):
            part = 0.5 * (square[3 * k : 3 * k + 1] + square[3 * k + 1 : 3 * k + 2] + square[3 * k + 2 : 3 * k + 3])
            norms = jnp.where(row16 == 12 + k, part, norms)
        parts = split3(norms)
        wide_parts = [x.astype(F32) for x in parts]
        ones = [jnp.where(feature, x, 1.0) for x in wide_parts]
        stack = jnp.concatenate(
            [wide_parts[0], wide_parts[1], ones[0], ones[1], wide_parts[2], ones[0], jnp.zeros((32, TILE), F32)], axis=0
        )
        a_side[u] = jnp.transpose(stack).astype(BF16)
        weight = block[12:13]
        g_high, g_low = split2(jnp.where(feature, block * weight, weight))
        g_side[u] = jnp.concatenate([g_high, g_low], axis=0)
        if not with_own:
            return None
        h, m, l = wide_parts

        def own_block(left, right):
            return jnp.where(feature, left, right)

        minus = -jnp.ones_like(h)

        def shift(x):
            return -x

        full = [
            own_block(h, minus),
            own_block(h, minus),
            own_block(m, shift(h)),
            own_block(m, shift(m)),
            own_block(h, minus),
            own_block(l, shift(l)),
        ]
        return full

    def masks():
        found = []
        for k in range(KEPT):
            keep = (row16 >= 3 * k) & (row16 < 3 * k + 3) | (row16 == 12 + k)
            found.append(keep)
        return found

    kept_rows = masks()

    def nonbonded(turn, halo):
        fulls = [sides(turn, GT + t, True) for t in range(tiles)]
        for copy in halo:
            copy.wait_recv()
        for u in list(range(GT)) + list(range(GT + tiles, 2 * GT + tiles)):
            sides(turn, u, False)
        found = []
        base = spot * tiles - GT
        count = total * tiles
        for t in range(tiles):
            rhs = []
            for kp in range(KEPT // 2):
                pair = []
                for k in (2 * kp, 2 * kp + 1):
                    blocks = [jnp.where(kept_rows[k], x, 0.0) for x in fulls[t]]
                    pair.append(jnp.concatenate(blocks + [jnp.zeros((32, TILE), F32)], axis=0))
                rhs.append(jnp.concatenate(pair, axis=1).astype(BF16))
            sums = [None] * (KEPT // 2)
            for j in range(NBR):
                where = jnp.minimum(lax.rem(nbr_s[j, tiles * me + t] - base + count, count), tiles + 2 * GT - 1)
                a = a_side[where]
                g = g_side[where]
                gg = jnp.concatenate([g, g], axis=1)
                for kp in range(KEPT // 2):
                    w = jnp.exp2(mm(a, rhs[kp]))
                    high, low = split2(w)
                    got = mm(gg, jnp.concatenate([high, low], axis=0))
                    sums[kp] = got if sums[kp] is None else sums[kp] + got
            block = ext[turn, GT + t]
            force = jnp.zeros((16, TILE), F32)
            for k in range(KEPT):
                both = sums[k // 2]
                both = both[0:16] + both[16:32]
                both = lanes(both, k % 2)
                force = jnp.where((row16 >= 3 * k) & (row16 < 3 * k + 3), block * both[12:13] - both, force)
            found.append(force * strengths[t])
        high, low = split2(jnp.concatenate(found, axis=1))
        return mm(wide_table, jnp.concatenate([high, high, low], axis=0))

    def bonded(current):
        forces = []
        for t in range(tiles):
            high, low = split2(jnp.concatenate([lanes(x, t) for x in current], axis=0))
            table = pick[t]
            got = mm(jnp.concatenate([high, low], axis=1), jnp.concatenate([table, table], axis=0))
            stretch = [got[c * BEADS : (c + 1) * BEADS, :TILE] for c in range(3)]
            arms = [got[c * BEADS : (c + 1) * BEADS, TILE:] for c in range(3)]
            swapped = [pltpu.roll(x, APT, 1) for x in arms]
            factor = -bond_stiff * (sum(x * x for x in stretch) - bond_rest)
            bend = -angle_stiff * (sum(x * y for x, y in zip(arms, swapped)) - angle_rest)
            push = jnp.concatenate(
                [jnp.concatenate([factor * x, bend * y], axis=1) for x, y in zip(stretch, swapped)], axis=0
            )
            high, low = split2(push)
            back = drop[t]
            forces.append(mm(jnp.concatenate([high, low], axis=1), jnp.concatenate([back, back], axis=0)))
        return [
            jnp.concatenate([f[c * BEADS : (c + 1) * BEADS] for f in forces], axis=1) for c in range(3)
        ]

    def advance(current, speed):
        moved, fast = [], []
        for c in range(3):
            first = current[c][0:1]
            both = jnp.concatenate([current[c] - first, speed[c]], axis=0)
            high, low = split2(both)
            got = mm(free_table, jnp.concatenate([high, high, low], axis=0))
            moved.append(first + got[:BEADS])
            fast.append(got[BEADS:])
        return moved, fast

    half = 0.5 * time_step / SUBS

    local[2].wait()
    for copy in q_sends:
        copy.wait_recv()
    current = [q_all[c] for c in range(3)]
    halo = start_halo(0, contracted(current))
    pushed = bonded(current)
    kick = nonbonded(0, halo)
    halos = list(halo)
    kicks = [kick[c * BEADS : (c + 1) * BEADS] for c in range(3)]

    local[3].wait()
    for copy in p_sends:
        copy.wait_recv()
    speed = [(p_all[c] + half * pushed[c] + kicks[c]) * inverse for c in range(3)]
    for substep in range(SUBS):
        current, speed = advance(current, speed)
        if substep + 1 < SUBS:
            pushed = bonded(current)
            speed = [speed[c] + (2.0 * half) * pushed[c] * inverse for c in range(3)]

    halo = start_halo(1, contracted(current))
    halos = halos + list(halo)
    for c in range(3):
        q_done[c] = current[c]
    sends = sends + exchange(2, rows_of(q_done), q_out.at[:, :, my_lanes])
    mine_q = pltpu.make_async_copy(q_done.at[:, my_rows, :], q_out.at[:, :, my_lanes], own_sem.at[0])
    mine_q.start()
    pushed = bonded(current)
    moment = [speed[c] * mass_row + half * pushed[c] for c in range(3)]
    kick = nonbonded(1, halo)
    for c in range(3):
        p_done[c] = moment[c] + kick[c * BEADS : (c + 1) * BEADS]
    late = exchange(3, rows_of(p_done), p_out.at[:, :, my_lanes])
    mine_p = pltpu.make_async_copy(p_done.at[:, my_rows, :], p_out.at[:, :, my_lanes], own_sem.at[1])
    mine_p.start()
    for copy in sends:
        copy.wait_send()
    for copy in halos:
        copy.wait_send()
    for copy in sends[2 * (beads - 1) :]:
        copy.wait_recv()
    mine_q.wait()
    mine_p.wait()
    for copy in late:
        copy.wait()


def solution(mesh):
    spaces, beads = mesh.shape["space"], mesh.shape["bead"]
    table = constant_table()

    def body(positions, momenta, masses, strengths, bond_ends, angle_ends, neighbour_tiles):
        held, _, slab = positions.shape
        own = slab // beads
        tiles = own // TILE
        near = tiles + 2 * GT
        moved = jax.ShapeDtypeStruct((3, held, slab), F32)
        anywhere = pl.BlockSpec(memory_space=pl.ANY)
        done = pl.pallas_call(
            functools.partial(kernel, spaces, beads),
            out_shape=(moved, moved),
            in_specs=[anywhere] * 8,
            out_specs=(anywhere, anywhere),
            scratch_shapes=[
                pltpu.VMEM((3, held, slab), F32),
                pltpu.VMEM((3, held, slab), F32),
                pltpu.VMEM((3, BEADS, own), F32),
                pltpu.VMEM((3, BEADS, own), F32),
                pltpu.VMEM((3, BEADS, own), F32),
                pltpu.VMEM((3, BEADS, own), F32),
                pltpu.VMEM((slab // TILE, TILE), F32),
                pltpu.VMEM((slab // TILE, TILE), F32),
                pltpu.VMEM((2, own), jnp.int32),
                pltpu.VMEM((3, own // 2), jnp.int32),
                pltpu.SMEM((NBR, slab // TILE), jnp.int32),
                pltpu.VMEM(table.shape, BF16),
                pltpu.VMEM((tiles, TILE, 2 * TILE), BF16),
                pltpu.VMEM((tiles, 2 * TILE, TILE), BF16),
                pltpu.VMEM((2, near, 16, TILE), F32),
                pltpu.VMEM((near, TILE, TILE), BF16),
                pltpu.VMEM((near, 32, TILE), BF16),
                pltpu.SemaphoreType.DMA((10,)),
                pltpu.SemaphoreType.DMA((4, beads - 1)),
                pltpu.SemaphoreType.DMA((4, beads - 1)),
                pltpu.SemaphoreType.DMA((2,)),
                pltpu.SemaphoreType.DMA((2, 2)),
                pltpu.SemaphoreType.DMA((2, 2)),
            ],
            compiler_params=pltpu.CompilerParams(collective_id=0, has_side_effects=True),
        )(
            jnp.transpose(positions, (1, 0, 2)),
            jnp.transpose(momenta, (1, 0, 2)),
            masses.reshape(-1, TILE),
            strengths.reshape(-1, TILE),
            bond_ends,
            angle_ends,
            neighbour_tiles,
            jnp.asarray(table),
        )
        return tuple(jnp.transpose(x, (1, 0, 2)) for x in done)

    placed = (
        P("bead", None, "space"),
        P("bead", None, "space"),
        P("space"),
        P("space"),
        P(None, "space"),
        P(None, "space"),
        P(None, "space"),
    )
    return jax.shard_map(
        body,
        mesh=mesh,
        in_specs=placed,
        out_specs=(P("bead", None, "space"), P("bead", None, "space")),
        check_vma=False,
    )
```

time: 112 us -> 36.5 us (0.33); the launches traced: 110 us -> 36.1 us
  starting transfers between devices: 45.6 us -> 0 us
  Pallas kernels: 0 us -> 33.2 us
  matrix products: 32.6 us -> 0 us
  waiting for transfers between devices: 13.6 us -> 0 us
  local copies, waits for them, and re-layouts: 13.3 us -> 2.34 us
  other arithmetic: 3.39 us -> 0 us
    all_to_all x6 -> x0, starting transfers between devices: 39.6 us -> none  [the longest x4 24.7 us: several_exchanges(): lax.all_to_all(section, axis, split_axis=0, concat_axis=0, tiled=True)]
    pallas_call x0 -> x1, Pallas kernels: none -> 33.2 us  [body(): pl.pallas_call(functools.partial(kernel, spaces, beads), out_shape=(moved...]
    dot_general x60 -> x0, matrix products: 32.6 us -> none  [the longest x2 9.02 us: pair_block(): inner = jnp.einsum('cxta,cxtn->ctan', own_tiles, nearby, precision=HIGH)]
    all_to_all x6 -> x0, waiting for transfers between devices: 13.6 us -> none  [the longest x4 8.98 us: several_exchanges(): lax.all_to_all(section, axis, split_axis=0, concat_axis=0, tiled=True)]
    ppermute x4 -> x0, starting transfers between devices: 6.01 us -> none  [the longest x2 3.55 us: padded(): lax.ppermute(leading, axis, [(b, a) for a, b in up])]
    split x6 -> x0, local copies, waits for them, and re-layouts: 2.88 us -> none  [several_exchanges(): jnp.split(parts, edges_of(parts.shape[split_at], pieces), axis=split_at)]
    reshape x9 -> x0, local copies, waits for them, and re-layouts: 2.46 us -> none  [the longest x2 2.13 us: cut_along(): return jnp.moveaxis(array.reshape(*before, length, -1, *after), dim, 0)]
    gather x4 -> x0, local copies, waits for them, and re-layouts: 2.33 us -> none  [the longest x2 1.21 us: one_group(): jnp.take(tiled, chosen, axis=2).reshape(kept, 3, group_size, width * TILE)]
  transfers between devices with their start and end apart: 10 -> 0, of which waited for: 3 -> 0; matrix products, arithmetic and copies ran while one was open for 21% -> 0% of each run, Pallas kernels for 0% -> 0%
where the time goes in v1:
time: 36.5 us; the launch traced here: 36.1 us
  Pallas kernels  33.2 us (91%)
  local copies, waits for them, and re-layouts  2.34 us (6%)
  between operations  0.65 us (2%)
    pallas_call x1, Pallas kernels, body(): pl.pallas_call(functools.partial(kernel, spaces, beads), out_shape=(moved...  33.2 us
    unnamed x4, local copies, waits for them, and re-layouts  2.34 us

profile of v1, /device:TPU:8, one launch (start us, length us, event | category | flops | bytes accessed | tf_op | source)
XLA Modules:
  0.0 36.1 jit_solution(16508012280780484967)
XLA Ops:
  0.6 33.2 %shard_map.95 = (f32[3,4,4096]{2,1,0:T(4,128)}, f32[3,4,4096]{2,1,0:T(4,128)}) custom-call(f32[3,4,4096]{2,1,0:T(4,128)} %bitcast.6, f32[3,4,4096]{2,1,0:T(4,128)} %bitcast.7, f32[32,128]{1,0:T(8,128)} %bitcast.10, f32[32,128]{1,0:T(8,128)} %bitcast.11, s32[2,4096]{1,0:T(2,128)} %bond_in.1, s32[3,2048]{1,0:T(4,128)} %angle_in.1, s32[3,32]{1,0:T(4,128)} %nbr_in.1, ...), custom_call_target="tpu_custom_call" | custom-call | tf_op jit(solution)/shard_map/pallas_call | solution.py:467
  33.8 0.0 copy-start
  33.8 1.7 %copy.12 = f32[4,3,4096]{2,0,1:T(4,128)} copy(f32[4,3,4096]{2,0,1:T(4,128)} %bitcast.9) | data formatting | bytes 393216
  35.5 0.0 copy-done
  35.5 0.7 %copy.13 = f32[4,3,4096]{2,0,1:T(4,128)} copy(f32[4,3,4096]{2,0,1:T(4,128)S(1)} %bitcast.8) | data formatting | bytes 393216
Async XLA Ops:
  33.8 1.7 %copy-start = (f32[3,4,4096]{2,1,0:T(4,128)S(1)}, f32[3,4,4096]{2,1,0:T(4,128)}, u32[]{:S(2)}) copy-start(f32[3,4,4096]{2,1,0:T(4,128)} %get-tuple-element.5) | copy-start | bytes 589828

commit v2 on v1

--- a/solution.py
+++ b/solution.py
@@ -113,6 +113,27 @@
 
 def lanes(x, t):
     return x[:, t * TILE : (t + 1) * TILE]
+
+
+def walk(space, place, beads):
+    core = lax.rem(space, 2)
+    return core * (beads - 1) + (1 - 2 * core) * place
+
+
+def flip(space):
+    return 1 - lax.rem(lax.div(space, 2), 2)
+
+
+def block_of(space, bead, beads):
+    row = lax.div(bead, 2)
+    return walk(space, 2 * row + lax.rem(bead + row + flip(space), 2), beads)
+
+
+def device_of(spot, beads):
+    space = lax.div(spot, beads)
+    place = walk(space, lax.rem(spot, beads), beads)
+    row = lax.div(place, 2)
+    return space, 2 * row + lax.rem(place + row + flip(space), 2)
 
 
 def kernel(
@@ -159,11 +180,10 @@
     tiles = own // TILE
     held = q_in.shape[1]
     total = spaces * beads
-    spot = space * beads + me
-    after = lax.rem(spot + 1, total)
-    before = lax.rem(spot + total - 1, total)
-    after_id = (lax.div(after, beads), lax.rem(after, beads))
-    before_id = (lax.div(before, beads), lax.rem(before, beads))
+    block = block_of(space, me, beads)
+    spot = space * beads + block
+    after_id = device_of(lax.rem(spot + 1, total), beads)
+    before_id = device_of(lax.rem(spot + total - 1, total), beads)
     peers = [lax.rem(me + d, beads) for d in range(1, beads)]
     order = sorted(range(beads - 1), key=lambda n: -min(n + 1, beads - n - 1))
 
@@ -174,14 +194,14 @@
         pl.semaphore_signal(barrier, inc=1, device_id=device, device_id_type=MESH)
 
     my_rows = pl.ds(pl.multiple_of(held * me, held), held)
-    my_lanes = pl.ds(pl.multiple_of(own * me, own), own)
+    my_lanes = pl.ds(pl.multiple_of(own * block, own), own)
     local = [
         (q_in, q_stage),
         (p_in, p_stage),
         (q_in.at[:, :, my_lanes], q_all.at[:, my_rows, :]),
         (p_in.at[:, :, my_lanes], p_all.at[:, my_rows, :]),
         (bond_in.at[:, my_lanes], bond_v),
-        (angle_in.at[:, pl.ds(pl.multiple_of((own // 2) * me, own // 2), own // 2)], angle_v),
+        (angle_in.at[:, pl.ds(pl.multiple_of((own // 2) * block, own // 2), own // 2)], angle_v),
         (mass_in, mass_v),
         (strength_in, strength_v),
         (nbr_in, nbr_s),
@@ -210,7 +230,7 @@
         return copies
 
     def lanes_of(ref):
-        return lambda peer: ref.at[:, :, pl.ds(pl.multiple_of(own * peer, own), own)]
+        return lambda peer: ref.at[:, :, pl.ds(pl.multiple_of(own * block_of(space, peer, beads), own), own)]
 
     def rows_of(ref):
         return lambda peer: ref.at[:, pl.ds(pl.multiple_of(held * peer, held), held), :]
@@ -245,9 +265,9 @@
         pick[t] = jnp.concatenate([bonds, angles], axis=1).astype(BF16)
         drop[t] = jnp.concatenate([jnp.transpose(bonds), jnp.transpose(angles)], axis=0).astype(BF16)
 
-    mass_row = jnp.concatenate([mass_v[pl.ds(tiles * me + t, 1), :] for t in range(tiles)], axis=1)
+    mass_row = jnp.concatenate([mass_v[pl.ds(tiles * block + t, 1), :] for t in range(tiles)], axis=1)
     inverse = 1.0 / mass_row
-    strengths = [strength_v[pl.ds(tiles * me + t, 1), :] for t in range(tiles)]
+    strengths = [strength_v[pl.ds(tiles * block + t, 1), :] for t in range(tiles)]
 
     free_table = const_v[0:64, 0:192]
     narrow_table = const_v[64:80, 0:288]
@@ -285,8 +305,8 @@
     scale = math.sqrt(2.0 / range_sq * math.log2(math.e))
 
     def sides(turn, u, with_own):
-        block = ext[turn, u]
-        scaled = block * scale
+        rows = ext[turn, u]
+        scaled = rows * scale
         square = scaled * scaled
         norms = scaled
         for k in range(KEPT):
@@ -299,8 +319,8 @@
             [wide_parts[0], wide_parts[1], ones[0], ones[1], wide_parts[2], ones[0], jnp.zeros((32, TILE), F32)], axis=0
         )
         a_side[u] = jnp.transpose(stack).astype(BF16)
-        weight = block[12:13]
-        g_high, g_low = split2(jnp.where(feature, block * weight, weight))
+        weight = rows[12:13]
+        g_high, g_low = split2(jnp.where(feature, rows * weight, weight))
         g_side[u] = jnp.concatenate([g_high, g_low], axis=0)
         if not with_own:
             return None
@@ -352,7 +372,7 @@
                 rhs.append(jnp.concatenate(pair, axis=1).astype(BF16))
             sums = [None] * (KEPT // 2)
             for j in range(NBR):
-                where = jnp.minimum(lax.rem(nbr_s[j, tiles * me + t] - base + count, count), tiles + 2 * GT - 1)
+                where = jnp.minimum(lax.rem(nbr_s[j, tiles * block + t] - base + count, count), tiles + 2 * GT - 1)
                 a = a_side[where]
                 g = g_side[where]
                 gg = jnp.concatenate([g, g], axis=1)
@@ -361,13 +381,13 @@
                     high, low = split2(w)
                     got = mm(gg, jnp.concatenate([high, low], axis=0))
                     sums[kp] = got if sums[kp] is None else sums[kp] + got
-            block = ext[turn, GT + t]
+            rows = ext[turn, GT + t]
             force = jnp.zeros((16, TILE), F32)
             for k in range(KEPT):
                 both = sums[k // 2]
                 both = both[0:16] + both[16:32]
                 both = lanes(both, k % 2)
-                force = jnp.where((row16 >= 3 * k) & (row16 < 3 * k + 3), block * both[12:13] - both, force)
+                force = jnp.where((row16 >= 3 * k) & (row16 < 3 * k + 3), rows * both[12:13] - both, force)
             found.append(force * strengths[t])
         high, low = split2(jnp.concatenate(found, axis=1))
         return mm(wide_table, jnp.concatenate([high, high, low], axis=0))
@@ -462,13 +482,13 @@
         own = slab // beads
         tiles = own // TILE
         near = tiles + 2 * GT
-        moved = jax.ShapeDtypeStruct((3, held, slab), F32)
+        moved = pltpu.VMEM((3, held, slab), F32)
         anywhere = pl.BlockSpec(memory_space=pl.ANY)
         done = pl.pallas_call(
             functools.partial(kernel, spaces, beads),
             out_shape=(moved, moved),
             in_specs=[anywhere] * 8,
-            out_specs=(anywhere, anywhere),
+            out_specs=(pl.BlockSpec(memory_space=pltpu.VMEM),) * 2,
             scratch_shapes=[
                 pltpu.VMEM((3, held, slab), F32),
                 pltpu.VMEM((3, held, slab), F32),

time: 36.5 us -> 30.7 us (0.84)
  Pallas kernels: 33.2 us -> 28.5 us
  local copies, waits for them, and re-layouts: 2.34 us -> 1.36 us
    pallas_call x1, Pallas kernels: 33.2 us -> 28.5 us  [body(): pl.pallas_call(functools.partial(kernel, spaces, beads), out_shape=(moved...]
    unnamed x4 -> x2, local copies, waits for them, and re-layouts: 2.34 us -> 1.36 us
where the time goes in v2:
time: 30.7 us; the launch traced here: 30.5 us
  Pallas kernels  28.5 us (93%)
  local copies, waits for them, and re-layouts  1.36 us (4%)
  between operations  0.64 us (2%)
    pallas_call x1, Pallas kernels, body(): pl.pallas_call(functools.partial(kernel, spaces, beads), out_shape=(moved...  28.5 us
    unnamed x2, local copies, waits for them, and re-layouts  1.36 us

profile of v2, /device:TPU:8, one launch (start us, length us, event | category | flops | bytes accessed | tf_op | source)
XLA Modules:
  0.0 30.5 jit_solution(15059384968044677717)
XLA Ops:
  0.6 28.5 %shard_map.95 = (f32[3,4,4096]{2,1,0:T(4,128)S(1)}, f32[3,4,4096]{2,1,0:T(4,128)S(1)}) custom-call(f32[3,4,4096]{2,1,0:T(4,128)} %bitcast.8, f32[3,4,4096]{2,1,0:T(4,128)} %bitcast.9, f32[32,128]{1,0:T(8,128)} %bitcast.10, f32[32,128]{1,0:T(8,128)} %bitcast.11, s32[2,4096]{1,0:T(2,128)} %bond_in.1, s32[3,2048]{1,0:T(4,128)} %angle_in.1, s32[3,32]{1,0:T(4,128)} %nbr_in.1, ...), custom_call_target="tpu_custom_call" | custom-call | tf_op jit(solution)/shard_map/pallas_call | solution.py:487
  29.1 0.7 %copy.12 = f32[4,3,4096]{2,0,1:T(4,128)} copy(f32[4,3,4096]{2,0,1:T(4,128)S(1)} %bitcast.7) | data formatting | bytes 393216
  29.8 0.7 %copy.13 = f32[4,3,4096]{2,0,1:T(4,128)} copy(f32[4,3,4096]{2,0,1:T(4,128)S(1)} %bitcast.6) | data formatting | bytes 393216

commit v3 on v2

--- a/solution.py
+++ b/solution.py
@@ -26,6 +26,8 @@
 angle_stiff = 0.1
 angle_rest = 0.5
 range_sq = 4.0
+CHUNK = 2
+GROUP = 4
 
 F32 = jnp.float32
 BF16 = jnp.bfloat16
@@ -187,6 +189,8 @@
     peers = [lax.rem(me + d, beads) for d in range(1, beads)]
     order = sorted(range(beads - 1), key=lambda n: -min(n + 1, beads - n - 1))
 
+    early = pltpu.make_async_copy(q_in, q_stage, local_sem.at[0])
+    early.start()
     barrier = pltpu.get_barrier_semaphore()
     for peer in peers:
         pl.semaphore_signal(barrier, inc=1, device_id=(space, peer), device_id_type=MESH)
@@ -208,7 +212,7 @@
         (const_in, const_v),
     ]
     local = [pltpu.make_async_copy(a, b, local_sem.at[n]) for n, (a, b) in enumerate(local)]
-    for copy in local:
+    for copy in local[1:]:
         copy.start()
 
     def exchange(kind, source, target):
@@ -353,49 +357,49 @@
 
     kept_rows = masks()
 
-    def nonbonded(turn, halo):
+    def prepare(turn, halo):
         fulls = [sides(turn, GT + t, True) for t in range(tiles)]
         for copy in halo:
             copy.wait_recv()
         for u in list(range(GT)) + list(range(GT + tiles, 2 * GT + tiles)):
             sides(turn, u, False)
-        found = []
+        return fulls
+
+    def nonbonded(turn, fulls, finish, chosen):
         base = spot * tiles - GT
         count = total * tiles
-        for t in range(tiles):
-            rhs = []
+        for t in chosen:
+            near = [
+                jnp.minimum(lax.rem(nbr_s[j, tiles * block + t] - base + count, count), tiles + 2 * GT - 1)
+                for j in range(NBR)
+            ]
+            a = jnp.concatenate([a_side[u] for u in near], axis=0)
+            g = [g_side[u] for u in near]
+            g = jnp.concatenate([x for x in g for _ in range(2)], axis=1)
+            rows = ext[turn, GT + t]
+            force = jnp.zeros((16, TILE), F32)
             for kp in range(KEPT // 2):
                 pair = []
                 for k in (2 * kp, 2 * kp + 1):
                     blocks = [jnp.where(kept_rows[k], x, 0.0) for x in fulls[t]]
                     pair.append(jnp.concatenate(blocks + [jnp.zeros((32, TILE), F32)], axis=0))
-                rhs.append(jnp.concatenate(pair, axis=1).astype(BF16))
-            sums = [None] * (KEPT // 2)
-            for j in range(NBR):
-                where = jnp.minimum(lax.rem(nbr_s[j, tiles * block + t] - base + count, count), tiles + 2 * GT - 1)
-                a = a_side[where]
-                g = g_side[where]
-                gg = jnp.concatenate([g, g], axis=1)
-                for kp in range(KEPT // 2):
-                    w = jnp.exp2(mm(a, rhs[kp]))
-                    high, low = split2(w)
-                    got = mm(gg, jnp.concatenate([high, low], axis=0))
-                    sums[kp] = got if sums[kp] is None else sums[kp] + got
-            rows = ext[turn, GT + t]
-            force = jnp.zeros((16, TILE), F32)
-            for k in range(KEPT):
-                both = sums[k // 2]
-                both = both[0:16] + both[16:32]
-                both = lanes(both, k % 2)
-                force = jnp.where((row16 >= 3 * k) & (row16 < 3 * k + 3), rows * both[12:13] - both, force)
-            found.append(force * strengths[t])
-        high, low = split2(jnp.concatenate(found, axis=1))
-        return mm(wide_table, jnp.concatenate([high, high, low], axis=0))
-
-    def bonded(current):
+                rhs = jnp.concatenate(pair, axis=1).astype(BF16)
+                weights = jnp.exp2(mm(a, rhs))
+                stack = []
+                for j in range(NBR):
+                    stack.extend(split2(weights[j * TILE : (j + 1) * TILE]))
+                got = mm(g, jnp.concatenate(stack, axis=0))
+                got = got[0:16] + got[16:32]
+                for k in (2 * kp, 2 * kp + 1):
+                    both = lanes(got, k % 2)
+                    force = jnp.where((row16 >= 3 * k) & (row16 < 3 * k + 3), rows * both[12:13] - both, force)
+            high, low = split2(force * strengths[t])
+            finish(t, mm(wide_table, jnp.concatenate([high, high, low], axis=0)))
+
+    def bonded(current, chosen):
         forces = []
-        for t in range(tiles):
-            high, low = split2(jnp.concatenate([lanes(x, t) for x in current], axis=0))
+        for n, t in enumerate(chosen):
+            high, low = split2(jnp.concatenate([lanes(x, n) for x in current], axis=0))
             table = pick[t]
             got = mm(jnp.concatenate([high, low], axis=1), jnp.concatenate([table, table], axis=0))
             stretch = [got[c * BEADS : (c + 1) * BEADS, :TILE] for c in range(3)]
@@ -431,20 +435,37 @@
         copy.wait_recv()
     current = [q_all[c] for c in range(3)]
     halo = start_halo(0, contracted(current))
-    pushed = bonded(current)
-    kick = nonbonded(0, halo)
     halos = list(halo)
-    kicks = [kick[c * BEADS : (c + 1) * BEADS] for c in range(3)]
+    everything = list(range(tiles))
+    pushed = bonded(current, everything)
+    kicks = [None] * tiles
+
+    def keep(t, kick):
+        kicks[t] = kick
 
     local[3].wait()
     for copy in p_sends:
         copy.wait_recv()
-    speed = [(p_all[c] + half * pushed[c] + kicks[c]) * inverse for c in range(3)]
-    for substep in range(SUBS):
-        current, speed = advance(current, speed)
-        if substep + 1 < SUBS:
-            pushed = bonded(current)
-            speed = [speed[c] + (2.0 * half) * pushed[c] * inverse for c in range(3)]
+    fulls = prepare(0, halo)
+    ended = []
+    for first in range(0, tiles, GROUP):
+        chosen = everything[first : first + GROUP]
+        span = slice(first * TILE, (first + GROUP) * TILE)
+        nonbonded(0, fulls, keep, chosen)
+        kick = jnp.concatenate([kicks[t] for t in chosen], axis=1)
+        inv = inverse[:, span]
+        here = [x[:, span] for x in current]
+        speed = [
+            (p_all[c, :, span] + half * pushed[c][:, span] + kick[c * BEADS : (c + 1) * BEADS]) * inv for c in range(3)
+        ]
+        for substep in range(SUBS):
+            here, speed = advance(here, speed)
+            if substep + 1 < SUBS:
+                force = bonded(here, chosen)
+                speed = [speed[c] + (2.0 * half) * force[c] * inv for c in range(3)]
+        ended.append((here, speed))
+    current = [jnp.concatenate([e[0][c] for e in ended], axis=1) for c in range(3)]
+    speed = [jnp.concatenate([e[1][c] for e in ended], axis=1) for c in range(3)]
 
     halo = start_halo(1, contracted(current))
     halos = halos + list(halo)
@@ -453,23 +474,55 @@
     sends = sends + exchange(2, rows_of(q_done), q_out.at[:, :, my_lanes])
     mine_q = pltpu.make_async_copy(q_done.at[:, my_rows, :], q_out.at[:, :, my_lanes], own_sem.at[0])
     mine_q.start()
-    pushed = bonded(current)
+    pushed = bonded(current, everything)
     moment = [speed[c] * mass_row + half * pushed[c] for c in range(3)]
-    kick = nonbonded(1, halo)
-    for c in range(3):
-        p_done[c] = moment[c] + kick[c * BEADS : (c + 1) * BEADS]
-    late = exchange(3, rows_of(p_done), p_out.at[:, :, my_lanes])
-    mine_p = pltpu.make_async_copy(p_done.at[:, my_rows, :], p_out.at[:, :, my_lanes], own_sem.at[1])
-    mine_p.start()
+    late = []
+
+    def send_home(t, kick):
+        spans = slice(t * TILE, (t + 1) * TILE)
+        for c in range(3):
+            p_done[c, :, spans] = lanes(moment[c], t) + kick[c * BEADS : (c + 1) * BEADS]
+        if (t + 1) % CHUNK:
+            return
+        width = CHUNK * TILE
+        begin = (t + 1 - CHUNK) * TILE
+        here = pl.ds(pl.multiple_of(own * block + begin, TILE), width)
+        target = p_out.at[:, :, here]
+        for n in order:
+            rows = pl.ds(pl.multiple_of(held * peers[n], held), held)
+            copy = pltpu.make_async_remote_copy(
+                src_ref=p_done.at[:, rows, begin : begin + width],
+                dst_ref=target,
+                send_sem=send_sem.at[3 + t // CHUNK, n],
+                recv_sem=recv_sem.at[3 + t // CHUNK, n],
+                device_id=(space, peers[n]),
+                device_id_type=MESH,
+            )
+            copy.start()
+            late.append(copy)
+        mine = pltpu.make_async_copy(p_done.at[:, my_rows, begin : begin + width], target, own_sem.at[1 + t // CHUNK])
+        mine.start()
+        late.append(mine)
+
+    nonbonded(1, prepare(1, halo), send_home, everything)
     for copy in sends:
         copy.wait_send()
     for copy in halos:
         copy.wait_send()
-    for copy in sends[2 * (beads - 1) :]:
+    for copy in sends[(2) * (beads - 1) :]:
         copy.wait_recv()
     mine_q.wait()
-    mine_p.wait()
     for copy in late:
+        copy.wait()
+
+
+def put_out(q_ref, p_ref, q_out, p_out, sem):
+    copies = [
+        pltpu.make_async_copy(a, b, sem.at[n]) for n, (a, b) in enumerate(((q_ref, q_out), (p_ref, p_out)))
+    ]
+    for copy in copies:
+        copy.start()
+    for copy in copies:
         copy.wait()
 
 
@@ -508,9 +561,9 @@
                 pltpu.VMEM((near, TILE, TILE), BF16),
                 pltpu.VMEM((near, 32, TILE), BF16),
                 pltpu.SemaphoreType.DMA((10,)),
-                pltpu.SemaphoreType.DMA((4, beads - 1)),
-                pltpu.SemaphoreType.DMA((4, beads - 1)),
-                pltpu.SemaphoreType.DMA((2,)),
+                pltpu.SemaphoreType.DMA((3 + tiles, beads - 1)),
+                pltpu.SemaphoreType.DMA((3 + tiles, beads - 1)),
+                pltpu.SemaphoreType.DMA((1 + tiles,)),
                 pltpu.SemaphoreType.DMA((2, 2)),
                 pltpu.SemaphoreType.DMA((2, 2)),
             ],
@@ -525,6 +578,15 @@
             neighbour_tiles,
             jnp.asarray(table),
         )
+        done = [pltpu.with_memory_space_constraint(x, pltpu.VMEM) for x in done]
+        plain = jax.ShapeDtypeStruct((3, held, slab), F32)
+        done = pl.pallas_call(
+            put_out,
+            out_shape=(plain, plain),
+            in_specs=[anywhere] * 2,
+            out_specs=(anywhere, anywhere),
+            scratch_shapes=[pltpu.SemaphoreType.DMA((2,))],
+        )(*done)
         return tuple(jnp.transpose(x, (1, 0, 2)) for x in done)
 
     placed = (

time: 30.7 us -> 29.1 us (0.948)
  local copies, waits for them, and re-layouts: 1.36 us -> 0 us
    unnamed x2 -> x0, local copies, waits for them, and re-layouts: 1.36 us -> none
    pallas_call x1, Pallas kernels: 28.5 us -> 27.6 us  [body(): pl.pallas_call(functools.partial(kernel, spaces, beads), out_shape=(moved...]
    pallas_call x0 -> x1, Pallas kernels: none -> 0.76 us  [body(): pl.pallas_call(put_out, out_shape=(plain, plain), in_specs=[anywhere] * 2...]
where the time goes in v3:
time: 29.1 us; the launch traced here: 29 us
  Pallas kernels  28.3 us (97%)
  between operations  0.64 us (2%)
    pallas_call x1, Pallas kernels, body(): pl.pallas_call(functools.partial(kernel, spaces, beads), out_shape=(moved...  27.6 us
    pallas_call x1, Pallas kernels, body(): pl.pallas_call(put_out, out_shape=(plain, plain), in_specs=[anywhere] * 2...  0.76 us

profile of v3, /device:TPU:8, one launch (start us, length us, event | category | flops | bytes accessed | tf_op | source)
XLA Modules:
  0.0 29.0 jit_solution(14312244059304741172)
XLA Ops:
  0.6 27.6 %shard_map.95 = (f32[3,4,4096]{2,1,0:T(4,128)S(1)}, f32[3,4,4096]{2,1,0:T(4,128)S(1)}) custom-call(f32[3,4,4096]{2,1,0:T(4,128)} %bitcast.6, f32[3,4,4096]{2,1,0:T(4,128)} %bitcast.7, f32[32,128]{1,0:T(8,128)} %bitcast.8, f32[32,128]{1,0:T(8,128)} %bitcast.9, s32[2,4096]{1,0:T(2,128)} %bond_in.1, s32[3,2048]{1,0:T(4,128)} %angle_in.1, s32[3,32]{1,0:T(4,128)} %nbr_in.1, ...), custom_call_target="tpu_custom_call" | custom-call | tf_op jit(solution)/shard_map/pallas_call | solution.py:540
  28.2 0.8 %shard_map.96 = (f32[3,4,4096]{2,1,0:T(4,128)}, f32[3,4,4096]{2,1,0:T(4,128)}) custom-call(f32[3,4,4096]{2,1,0:T(4,128)S(1)} %get-tuple-element.6.q_ref, f32[3,4,4096]{2,1,0:T(4,128)S(1)} %get-tuple-element.7.p_ref), custom_call_target="tpu_custom_call" | custom-call | tf_op jit(solution)/shard_map/pallas_call | solution.py:583

commit v4 on v3

--- a/solution.py
+++ b/solution.py
@@ -27,7 +27,6 @@
 angle_rest = 0.5
 range_sq = 4.0
 CHUNK = 2
-GROUP = 4
 
 F32 = jnp.float32
 BF16 = jnp.bfloat16
@@ -65,6 +64,11 @@
 def three_products(table):
     high, low = halves(table)
     return np.concatenate([high, low, high], axis=1)
+
+
+def stacked_rows(table):
+    high, low = halves(table)
+    return np.block([[high, high], [low, low]])
 
 
 def constant_table():
@@ -90,10 +94,13 @@
         for c in range(3):
             wide[c * BEADS : (c + 1) * BEADS, 3 * k + c] = expand[:, k]
     wide *= 0.5 * time_step * 2.0 / range_sq
-    table = np.zeros((64 + 16 + 96, 384), ml_dtypes.bfloat16)
-    table[:64, :192] = three_products(free)
-    table[64:80, :288] = three_products(narrow)
-    table[80:176, :48] = three_products(wide)
+    table = np.zeros((352, 256), ml_dtypes.bfloat16)
+    table[:128, :128] = stacked_rows(free)
+    for c in range(3):
+        near = narrow[:, c * BEADS : (c + 1) * BEADS] @ free[:BEADS]
+        table[128 + 32 * c : 160 + 32 * c, :128] = stacked_rows(near)
+    table[224:256, :192] = stacked_rows(narrow)
+    table[256:352, :48] = three_products(wide)
     return table
 
 
@@ -168,6 +175,7 @@
     ext,
     a_side,
     g_side,
+    own_side,
     local_sem,
     send_sem,
     recv_sem,
@@ -273,16 +281,19 @@
     inverse = 1.0 / mass_row
     strengths = [strength_v[pl.ds(tiles * block + t, 1), :] for t in range(tiles)]
 
-    free_table = const_v[0:64, 0:192]
-    narrow_table = const_v[64:80, 0:288]
-    wide_table = const_v[80:176, 0:48]
+    free_rows = const_v[0:128, 0:128]
+    near_rows = [const_v[128 + 32 * c : 160 + 32 * c, 0:128] for c in range(3)]
+    narrow_rows = const_v[224:256, 0:192]
+    wide_table = const_v[256:352, 0:48]
 
     row16 = lax.broadcasted_iota(jnp.int32, (16, TILE), 0)
     feature = row16 < 12
+    row_wide = lax.broadcasted_iota(jnp.int32, (16, own), 0)
 
     def contracted(current):
         high, low = split2(jnp.concatenate(current, axis=0))
-        return mm(narrow_table, jnp.concatenate([high, high, low], axis=0))
+        got = mm(narrow_rows, jnp.concatenate([high, low], axis=0))
+        return got[:16] + got[16:]
 
     def start_halo(turn, narrow):
         for t in range(tiles):
@@ -358,17 +369,23 @@
     kept_rows = masks()
 
     def prepare(turn, halo):
-        fulls = [sides(turn, GT + t, True) for t in range(tiles)]
+        for t in range(tiles):
+            full = sides(turn, GT + t, True)
+            parts = []
+            for k in range(KEPT):
+                blocks = [jnp.where(kept_rows[k], x, 0.0) for x in full]
+                parts.append(jnp.concatenate(blocks + [jnp.zeros((32, TILE), F32)], axis=0))
+            own_side[t] = jnp.concatenate(parts, axis=1).astype(BF16)
         for copy in halo:
             copy.wait_recv()
         for u in list(range(GT)) + list(range(GT + tiles, 2 * GT + tiles)):
             sides(turn, u, False)
-        return fulls
-
-    def nonbonded(turn, fulls, finish, chosen):
+
+    def nonbonded(turn, finish, chunk):
         base = spot * tiles - GT
         count = total * tiles
-        for t in chosen:
+        found = []
+        for t in range(tiles):
             near = [
                 jnp.minimum(lax.rem(nbr_s[j, tiles * block + t] - base + count, count), tiles + 2 * GT - 1)
                 for j in range(NBR)
@@ -377,31 +394,29 @@
             g = [g_side[u] for u in near]
             g = jnp.concatenate([x for x in g for _ in range(2)], axis=1)
             rows = ext[turn, GT + t]
+            weights = jnp.exp2(mm(a, own_side[t]))
+            stack = []
+            for j in range(NBR):
+                stack.extend(split2(weights[j * TILE : (j + 1) * TILE]))
+            got = mm(g, jnp.concatenate(stack, axis=0))
+            got = got[0:16] + got[16:32]
             force = jnp.zeros((16, TILE), F32)
-            for kp in range(KEPT // 2):
-                pair = []
-                for k in (2 * kp, 2 * kp + 1):
-                    blocks = [jnp.where(kept_rows[k], x, 0.0) for x in fulls[t]]
-                    pair.append(jnp.concatenate(blocks + [jnp.zeros((32, TILE), F32)], axis=0))
-                rhs = jnp.concatenate(pair, axis=1).astype(BF16)
-                weights = jnp.exp2(mm(a, rhs))
-                stack = []
-                for j in range(NBR):
-                    stack.extend(split2(weights[j * TILE : (j + 1) * TILE]))
-                got = mm(g, jnp.concatenate(stack, axis=0))
-                got = got[0:16] + got[16:32]
-                for k in (2 * kp, 2 * kp + 1):
-                    both = lanes(got, k % 2)
-                    force = jnp.where((row16 >= 3 * k) & (row16 < 3 * k + 3), rows * both[12:13] - both, force)
-            high, low = split2(force * strengths[t])
-            finish(t, mm(wide_table, jnp.concatenate([high, high, low], axis=0)))
+            for k in range(KEPT):
+                both = lanes(got, k)
+                force = jnp.where((row16 >= 3 * k) & (row16 < 3 * k + 3), rows * both[12:13] - both, force)
+            found.append(force * strengths[t])
+            if len(found) == chunk:
+                high, low = split2(jnp.concatenate(found, axis=1))
+                found = []
+                finish(t, mm(wide_table, jnp.concatenate([high, high, low], axis=0)))
 
     def bonded(current, chosen):
         forces = []
         for n, t in enumerate(chosen):
             high, low = split2(jnp.concatenate([lanes(x, n) for x in current], axis=0))
             table = pick[t]
-            got = mm(jnp.concatenate([high, low], axis=1), jnp.concatenate([table, table], axis=0))
+            got = mm(jnp.concatenate([high, low], axis=0), table)
+            got = got[: 3 * BEADS] + got[3 * BEADS :]
             stretch = [got[c * BEADS : (c + 1) * BEADS, :TILE] for c in range(3)]
             arms = [got[c * BEADS : (c + 1) * BEADS, TILE:] for c in range(3)]
             swapped = [pltpu.roll(x, APT, 1) for x in arms]
@@ -412,21 +427,29 @@
             )
             high, low = split2(push)
             back = drop[t]
-            forces.append(mm(jnp.concatenate([high, low], axis=1), jnp.concatenate([back, back], axis=0)))
+            got = mm(jnp.concatenate([high, low], axis=0), back)
+            forces.append(got[: 3 * BEADS] + got[3 * BEADS :])
         return [
             jnp.concatenate([f[c * BEADS : (c + 1) * BEADS] for f in forces], axis=1) for c in range(3)
         ]
 
-    def advance(current, speed):
+    def advance(current, speed, last=False):
         moved, fast = [], []
+        narrow = None
         for c in range(3):
             first = current[c][0:1]
             both = jnp.concatenate([current[c] - first, speed[c]], axis=0)
             high, low = split2(both)
-            got = mm(free_table, jnp.concatenate([high, high, low], axis=0))
+            table = jnp.concatenate([free_rows, near_rows[c]], axis=0) if last else free_rows
+            got = mm(table, jnp.concatenate([high, low], axis=0))
+            if last:
+                part = got[4 * BEADS : 4 * BEADS + 16] + got[4 * BEADS + 16 :]
+                part = part + jnp.where(lax.rem(row_wide, 3) == c, first, 0.0)
+                narrow = part if narrow is None else narrow + part
+            got = got[: 2 * BEADS] + got[2 * BEADS : 4 * BEADS]
             moved.append(first + got[:BEADS])
             fast.append(got[BEADS:])
-        return moved, fast
+        return moved, fast, narrow
 
     half = 0.5 * time_step / SUBS
 
@@ -438,36 +461,26 @@
     halos = list(halo)
     everything = list(range(tiles))
     pushed = bonded(current, everything)
-    kicks = [None] * tiles
+    kicks = []
 
     def keep(t, kick):
-        kicks[t] = kick
+        kicks.append(kick)
 
     local[3].wait()
     for copy in p_sends:
         copy.wait_recv()
-    fulls = prepare(0, halo)
-    ended = []
-    for first in range(0, tiles, GROUP):
-        chosen = everything[first : first + GROUP]
-        span = slice(first * TILE, (first + GROUP) * TILE)
-        nonbonded(0, fulls, keep, chosen)
-        kick = jnp.concatenate([kicks[t] for t in chosen], axis=1)
-        inv = inverse[:, span]
-        here = [x[:, span] for x in current]
-        speed = [
-            (p_all[c, :, span] + half * pushed[c][:, span] + kick[c * BEADS : (c + 1) * BEADS]) * inv for c in range(3)
-        ]
-        for substep in range(SUBS):
-            here, speed = advance(here, speed)
-            if substep + 1 < SUBS:
-                force = bonded(here, chosen)
-                speed = [speed[c] + (2.0 * half) * force[c] * inv for c in range(3)]
-        ended.append((here, speed))
-    current = [jnp.concatenate([e[0][c] for e in ended], axis=1) for c in range(3)]
-    speed = [jnp.concatenate([e[1][c] for e in ended], axis=1) for c in range(3)]
-
-    halo = start_halo(1, contracted(current))
+    prepare(0, halo)
+    nonbonded(0, keep, tiles)
+    kick = kicks[0]
+    speed = [
+        (p_all[c] + half * pushed[c] + kick[c * BEADS : (c + 1) * BEADS]) * inverse for c in range(3)
+    ]
+    for substep in range(SUBS - 1):
+        current, speed, _ = advance(current, speed)
+        force = bonded(current, everything)
+        speed = [speed[c] + (2.0 * half) * force[c] * inverse for c in range(3)]
+    current, speed, narrow = advance(current, speed, True)
+    halo = start_halo(1, narrow)
     halos = halos + list(halo)
     for c in range(3):
         q_done[c] = current[c]
@@ -479,13 +492,12 @@
     late = []
 
     def send_home(t, kick):
-        spans = slice(t * TILE, (t + 1) * TILE)
-        for c in range(3):
-            p_done[c, :, spans] = lanes(moment[c], t) + kick[c * BEADS : (c + 1) * BEADS]
-        if (t + 1) % CHUNK:
-            return
         width = CHUNK * TILE
         begin = (t + 1 - CHUNK) * TILE
+        for c in range(3):
+            p_done[c, :, begin : begin + width] = (
+                moment[c][:, begin : begin + width] + kick[c * BEADS : (c + 1) * BEADS]
+            )
         here = pl.ds(pl.multiple_of(own * block + begin, TILE), width)
         target = p_out.at[:, :, here]
         for n in order:
@@ -504,7 +516,8 @@
         mine.start()
         late.append(mine)
 
-    nonbonded(1, prepare(1, halo), send_home, everything)
+    prepare(1, halo)
+    nonbonded(1, send_home, CHUNK)
     for copy in sends:
         copy.wait_send()
     for copy in halos:
@@ -560,6 +573,7 @@
                 pltpu.VMEM((2, near, 16, TILE), F32),
                 pltpu.VMEM((near, TILE, TILE), BF16),
                 pltpu.VMEM((near, 32, TILE), BF16),
+                pltpu.VMEM((tiles, TILE, KEPT * TILE), BF16),
                 pltpu.SemaphoreType.DMA((10,)),
                 pltpu.SemaphoreType.DMA((3 + tiles, beads - 1)),
                 pltpu.SemaphoreType.DMA((3 + tiles, beads - 1)),

time: 29.1 us -> 27.9 us (0.959)
  Pallas kernels: 28.3 us -> 27.2 us
    pallas_call x1, Pallas kernels: 27.6 us -> 26.4 us  [body(): pl.pallas_call(functools.partial(kernel, spaces, beads), out_shape=(moved...]
where the time goes in v4:
time: 27.9 us; the launch traced here: 27.8 us
  Pallas kernels  27.2 us (97%)
  between operations  0.64 us (2%)
    pallas_call x1, Pallas kernels, body(): pl.pallas_call(functools.partial(kernel, spaces, beads), out_shape=(moved...  26.4 us
    pallas_call x1, Pallas kernels, body(): pl.pallas_call(put_out, out_shape=(plain, plain), in_specs=[anywhere] * 2...  0.76 us

profile of v4, /device:TPU:8, one launch (start us, length us, event | category | flops | bytes accessed | tf_op | source)
XLA Modules:
  0.0 27.8 jit_solution(1844544284976689747)
XLA Ops:
  0.6 26.4 %shard_map.95 = (f32[3,4,4096]{2,1,0:T(4,128)S(1)}, f32[3,4,4096]{2,1,0:T(4,128)S(1)}) custom-call(f32[3,4,4096]{2,1,0:T(4,128)} %bitcast.6, f32[3,4,4096]{2,1,0:T(4,128)} %bitcast.7, f32[32,128]{1,0:T(8,128)} %bitcast.8, f32[32,128]{1,0:T(8,128)} %bitcast.9, s32[2,4096]{1,0:T(2,128)} %bond_in.1, s32[3,2048]{1,0:T(4,128)} %angle_in.1, s32[3,32]{1,0:T(4,128)} %nbr_in.1, ...), custom_call_target="tpu_custom_call" | custom-call | tf_op jit(solution)/shard_map/pallas_call | solution.py:553
  27.1 0.8 %shard_map.96 = (f32[3,4,4096]{2,1,0:T(4,128)}, f32[3,4,4096]{2,1,0:T(4,128)}) custom-call(f32[3,4,4096]{2,1,0:T(4,128)S(1)} %get-tuple-element.6.q_ref, f32[3,4,4096]{2,1,0:T(4,128)S(1)} %get-tuple-element.7.p_ref), custom_call_target="tpu_custom_call" | custom-call | tf_op jit(solution)/shard_map/pallas_call | solution.py:597

commit v5 on v4

--- a/solution.py
+++ b/solution.py
@@ -224,22 +224,19 @@
         copy.start()
 
     def exchange(kind, source, target):
-        copies = []
         for n in order:
-            peer = peers[n]
-            copies.append(
-                pltpu.make_async_remote_copy(
-                    src_ref=source(peer),
-                    dst_ref=target,
-                    send_sem=send_sem.at[kind, n],
-                    recv_sem=recv_sem.at[kind, n],
-                    device_id=(space, peer),
-                    device_id_type=MESH,
-                )
-            )
-        for copy in copies:
-            copy.start()
-        return copies
+            pltpu.make_async_remote_copy(
+                src_ref=source(peers[n]),
+                dst_ref=target,
+                send_sem=send_sem.at[kind],
+                recv_sem=recv_sem.at[kind],
+                device_id=(space, peers[n]),
+                device_id_type=MESH,
+            ).start()
+
+    def wait_all(sem):
+        sized = q_stage.at[:, :, pl.ds(0, (beads - 1) * own)]
+        pltpu.make_async_copy(sized, sized, sem).wait()
 
     def lanes_of(ref):
         return lambda peer: ref.at[:, :, pl.ds(pl.multiple_of(own * block_of(space, peer, beads), own), own)]
@@ -249,11 +246,9 @@
 
     pl.semaphore_wait(barrier, beads + 1)
     local[0].wait()
-    sends = exchange(0, lanes_of(q_stage), q_all.at[:, my_rows, :])
-    q_sends = list(sends)
+    exchange(0, lanes_of(q_stage), q_all.at[:, my_rows, :])
     local[1].wait()
-    p_sends = exchange(1, lanes_of(p_stage), p_all.at[:, my_rows, :])
-    sends = sends + p_sends
+    exchange(1, lanes_of(p_stage), p_all.at[:, my_rows, :])
 
     for n in (4, 5, 6, 7, 8, 9):
         local[n].wait()
@@ -298,24 +293,19 @@
     def start_halo(turn, narrow):
         for t in range(tiles):
             ext[turn, GT + t] = jnp.where(feature, lanes(narrow, t), strengths[t])
-        copies = []
-        for side, device, source, target in (
-            (0, before_id, GT, GT + tiles),
-            (1, after_id, tiles, 0),
-        ):
-            copies.append(
-                pltpu.make_async_remote_copy(
-                    src_ref=ext.at[turn, pl.ds(source, GT)],
-                    dst_ref=ext.at[turn, pl.ds(target, GT)],
-                    send_sem=halo_send.at[turn, side],
-                    recv_sem=halo_recv.at[turn, side],
-                    device_id=device,
-                    device_id_type=MESH,
-                )
-            )
-        for copy in copies:
-            copy.start()
-        return copies
+        for device, source, target in ((before_id, GT, GT + tiles), (after_id, tiles, 0)):
+            pltpu.make_async_remote_copy(
+                src_ref=ext.at[turn, pl.ds(source, GT)],
+                dst_ref=ext.at[turn, pl.ds(target, GT)],
+                send_sem=halo_send.at[turn],
+                recv_sem=halo_recv.at[turn],
+                device_id=device,
+                device_id_type=MESH,
+            ).start()
+
+    def wait_halo(sem):
+        both = ext.at[0, pl.ds(0, 2 * GT)]
+        pltpu.make_async_copy(both, both, sem).wait()
 
     scale = math.sqrt(2.0 / range_sq * math.log2(math.e))
 
@@ -368,7 +358,7 @@
 
     kept_rows = masks()
 
-    def prepare(turn, halo):
+    def prepare(turn):
         for t in range(tiles):
             full = sides(turn, GT + t, True)
             parts = []
@@ -376,8 +366,7 @@
                 blocks = [jnp.where(kept_rows[k], x, 0.0) for x in full]
                 parts.append(jnp.concatenate(blocks + [jnp.zeros((32, TILE), F32)], axis=0))
             own_side[t] = jnp.concatenate(parts, axis=1).astype(BF16)
-        for copy in halo:
-            copy.wait_recv()
+        wait_halo(halo_recv.at[turn])
         for u in list(range(GT)) + list(range(GT + tiles, 2 * GT + tiles)):
             sides(turn, u, False)
 
@@ -454,11 +443,9 @@
     half = 0.5 * time_step / SUBS
 
     local[2].wait()
-    for copy in q_sends:
-        copy.wait_recv()
+    wait_all(recv_sem.at[0])
     current = [q_all[c] for c in range(3)]
-    halo = start_halo(0, contracted(current))
-    halos = list(halo)
+    start_halo(0, contracted(current))
     everything = list(range(tiles))
     pushed = bonded(current, everything)
     kicks = []
@@ -467,9 +454,8 @@
         kicks.append(kick)
 
     local[3].wait()
-    for copy in p_sends:
-        copy.wait_recv()
-    prepare(0, halo)
+    wait_all(recv_sem.at[1])
+    prepare(0)
     nonbonded(0, keep, tiles)
     kick = kicks[0]
     speed = [
@@ -480,11 +466,10 @@
         force = bonded(current, everything)
         speed = [speed[c] + (2.0 * half) * force[c] * inverse for c in range(3)]
     current, speed, narrow = advance(current, speed, True)
-    halo = start_halo(1, narrow)
-    halos = halos + list(halo)
+    start_halo(1, narrow)
     for c in range(3):
         q_done[c] = current[c]
-    sends = sends + exchange(2, rows_of(q_done), q_out.at[:, :, my_lanes])
+    exchange(2, rows_of(q_done), q_out.at[:, :, my_lanes])
     mine_q = pltpu.make_async_copy(q_done.at[:, my_rows, :], q_out.at[:, :, my_lanes], own_sem.at[0])
     mine_q.start()
     pushed = bonded(current, everything)
@@ -502,31 +487,29 @@
         target = p_out.at[:, :, here]
         for n in order:
             rows = pl.ds(pl.multiple_of(held * peers[n], held), held)
-            copy = pltpu.make_async_remote_copy(
+            pltpu.make_async_remote_copy(
                 src_ref=p_done.at[:, rows, begin : begin + width],
                 dst_ref=target,
-                send_sem=send_sem.at[3 + t // CHUNK, n],
-                recv_sem=recv_sem.at[3 + t // CHUNK, n],
+                send_sem=send_sem.at[3],
+                recv_sem=recv_sem.at[3],
                 device_id=(space, peers[n]),
                 device_id_type=MESH,
-            )
-            copy.start()
-            late.append(copy)
+            ).start()
         mine = pltpu.make_async_copy(p_done.at[:, my_rows, begin : begin + width], target, own_sem.at[1 + t // CHUNK])
         mine.start()
         late.append(mine)
 
-    prepare(1, halo)
+    prepare(1)
     nonbonded(1, send_home, CHUNK)
-    for copy in sends:
-        copy.wait_send()
-    for copy in halos:
-        copy.wait_send()
-    for copy in sends[(2) * (beads - 1) :]:
-        copy.wait_recv()
+    for kind in range(4):
+        wait_all(send_sem.at[kind])
+    for turn in range(2):
+        wait_halo(halo_send.at[turn])
+    wait_all(recv_sem.at[2])
     mine_q.wait()
     for copy in late:
         copy.wait()
+    wait_all(recv_sem.at[3])
 
 
 def put_out(q_ref, p_ref, q_out, p_out, sem):
@@ -575,11 +558,11 @@
                 pltpu.VMEM((near, 32, TILE), BF16),
                 pltpu.VMEM((tiles, TILE, KEPT * TILE), BF16),
                 pltpu.SemaphoreType.DMA((10,)),
-                pltpu.SemaphoreType.DMA((3 + tiles, beads - 1)),
-                pltpu.SemaphoreType.DMA((3 + tiles, beads - 1)),
-                pltpu.SemaphoreType.DMA((1 + tiles,)),
-                pltpu.SemaphoreType.DMA((2, 2)),
-                pltpu.SemaphoreType.DMA((2, 2)),
+                pltpu.SemaphoreType.DMA((4,)),
+                pltpu.SemaphoreType.DMA((4,)),
+                pltpu.SemaphoreType.DMA((1 + tiles // CHUNK,)),
+                pltpu.SemaphoreType.DMA((2,)),
+                pltpu.SemaphoreType.DMA((2,)),
             ],
             compiler_params=pltpu.CompilerParams(collective_id=0, has_side_effects=True),
         )(

time: 27.9 us -> 27.1 us (0.971)
  Pallas kernels: 27.2 us -> 26.3 us
    pallas_call x1, Pallas kernels: 26.4 us -> 25.6 us  [body(): pl.pallas_call(functools.partial(kernel, spaces, beads), out_shape=(moved...]
where the time goes in v5:
time: 27.1 us; the launch traced here: 27 us
  Pallas kernels  26.3 us (97%)
  between operations  0.64 us (2%)
    pallas_call x1, Pallas kernels, body(): pl.pallas_call(functools.partial(kernel, spaces, beads), out_shape=(moved...  25.6 us
    pallas_call x1, Pallas kernels, body(): pl.pallas_call(put_out, out_shape=(plain, plain), in_specs=[anywhere] * 2...  0.76 us

profile of v5, /device:TPU:8, one launch (start us, length us, event | category | flops | bytes accessed | tf_op | source)
XLA Modules:
  0.0 27.0 jit_solution(6284129971990464386)
XLA Ops:
  0.6 25.6 %shard_map.95 = (f32[3,4,4096]{2,1,0:T(4,128)S(1)}, f32[3,4,4096]{2,1,0:T(4,128)S(1)}) custom-call(f32[3,4,4096]{2,1,0:T(4,128)} %bitcast.6, f32[3,4,4096]{2,1,0:T(4,128)} %bitcast.7, f32[32,128]{1,0:T(8,128)} %bitcast.8, f32[32,128]{1,0:T(8,128)} %bitcast.9, s32[2,4096]{1,0:T(2,128)} %bond_in.1, s32[3,2048]{1,0:T(4,128)} %angle_in.1, s32[3,32]{1,0:T(4,128)} %nbr_in.1, ...), custom_call_target="tpu_custom_call" | custom-call | tf_op jit(solution)/shard_map/pallas_call | solution.py:536
  26.2 0.8 %shard_map.96 = (f32[3,4,4096]{2,1,0:T(4,128)}, f32[3,4,4096]{2,1,0:T(4,128)}) custom-call(f32[3,4,4096]{2,1,0:T(4,128)S(1)} %get-tuple-element.6.q_ref, f32[3,4,4096]{2,1,0:T(4,128)S(1)} %get-tuple-element.7.p_ref), custom_call_target="tpu_custom_call" | custom-call | tf_op jit(solution)/shard_map/pallas_call | solution.py:580

commit v6 on v5

--- a/solution.py
+++ b/solution.py
@@ -94,13 +94,15 @@
         for c in range(3):
             wide[c * BEADS : (c + 1) * BEADS, 3 * k + c] = expand[:, k]
     wide *= 0.5 * time_step * 2.0 / range_sq
-    table = np.zeros((352, 256), ml_dtypes.bfloat16)
+    table = np.zeros((544, 256), ml_dtypes.bfloat16)
     table[:128, :128] = stacked_rows(free)
     for c in range(3):
         near = narrow[:, c * BEADS : (c + 1) * BEADS] @ free[:BEADS]
         table[128 + 32 * c : 160 + 32 * c, :128] = stacked_rows(near)
     table[224:256, :192] = stacked_rows(narrow)
     table[256:352, :48] = three_products(wide)
+    kicked = [free[:, BEADS:] @ wide[c * BEADS : (c + 1) * BEADS] for c in range(3)]
+    table[352:544, :48] = three_products(np.concatenate(kicked, axis=0))
     return table
 
 
@@ -198,7 +200,11 @@
     order = sorted(range(beads - 1), key=lambda n: -min(n + 1, beads - n - 1))
 
     early = pltpu.make_async_copy(q_in, q_stage, local_sem.at[0])
-    early.start()
+
+    @pl.when(me >= 0)
+    def _():
+        early.start()
+
     barrier = pltpu.get_barrier_semaphore()
     for peer in peers:
         pl.semaphore_signal(barrier, inc=1, device_id=(space, peer), device_id_type=MESH)
@@ -280,6 +286,7 @@
     near_rows = [const_v[128 + 32 * c : 160 + 32 * c, 0:128] for c in range(3)]
     narrow_rows = const_v[224:256, 0:192]
     wide_table = const_v[256:352, 0:48]
+    kick_table = const_v[352:544, 0:48]
 
     row16 = lax.broadcasted_iota(jnp.int32, (16, TILE), 0)
     feature = row16 < 12
@@ -395,9 +402,8 @@
                 force = jnp.where((row16 >= 3 * k) & (row16 < 3 * k + 3), rows * both[12:13] - both, force)
             found.append(force * strengths[t])
             if len(found) == chunk:
-                high, low = split2(jnp.concatenate(found, axis=1))
+                finish(t, jnp.concatenate(found, axis=1))
                 found = []
-                finish(t, mm(wide_table, jnp.concatenate([high, high, low], axis=0)))
 
     def bonded(current, chosen):
         forces = []
@@ -423,6 +429,16 @@
         ]
 
     def advance(current, speed, last=False):
+        if not last:
+            firsts = [x[0:1] for x in current]
+            both = jnp.concatenate(
+                [jnp.concatenate([x - f, y], axis=0) for x, f, y in zip(current, firsts, speed)], axis=1
+            )
+            high, low = split2(both)
+            got = mm(free_rows, jnp.concatenate([high, low], axis=0))
+            got = got[: 2 * BEADS] + got[2 * BEADS :]
+            got = [got[:, c * own : (c + 1) * own] for c in range(3)]
+            return [f + g[:BEADS] for f, g in zip(firsts, got)], [g[BEADS:] for g in got], None
         moved, fast = [], []
         narrow = None
         for c in range(3):
@@ -448,24 +464,25 @@
     start_halo(0, contracted(current))
     everything = list(range(tiles))
     pushed = bonded(current, everything)
-    kicks = []
-
-    def keep(t, kick):
-        kicks.append(kick)
-
     local[3].wait()
     wait_all(recv_sem.at[1])
+    speed = [(p_all[c] + half * pushed[c]) * inverse for c in range(3)]
+    current, speed, _ = advance(current, speed)
+    found = []
+
+    def keep(t, force):
+        found.append(force)
+
     prepare(0)
     nonbonded(0, keep, tiles)
-    kick = kicks[0]
-    speed = [
-        (p_all[c] + half * pushed[c] + kick[c * BEADS : (c + 1) * BEADS]) * inverse for c in range(3)
-    ]
-    for substep in range(SUBS - 1):
-        current, speed, _ = advance(current, speed)
+    high, low = split2(found[0] * inverse)
+    shift = mm(kick_table, jnp.concatenate([high, high, low], axis=0))
+    current = [x + shift[2 * BEADS * c : 2 * BEADS * c + BEADS] for c, x in enumerate(current)]
+    speed = [x + shift[2 * BEADS * c + BEADS : 2 * BEADS * (c + 1)] for c, x in enumerate(speed)]
+    for substep in range(1, SUBS):
         force = bonded(current, everything)
         speed = [speed[c] + (2.0 * half) * force[c] * inverse for c in range(3)]
-    current, speed, narrow = advance(current, speed, True)
+        current, speed, narrow = advance(current, speed, substep == SUBS - 1)
     start_halo(1, narrow)
     for c in range(3):
         q_done[c] = current[c]
@@ -476,7 +493,9 @@
     moment = [speed[c] * mass_row + half * pushed[c] for c in range(3)]
     late = []
 
-    def send_home(t, kick):
+    def send_home(t, force):
+        high, low = split2(force)
+        kick = mm(wide_table, jnp.concatenate([high, high, low], axis=0))
         width = CHUNK * TILE
         begin = (t + 1 - CHUNK) * TILE
         for c in range(3):

time: 27.1 us -> 26.9 us (level)
  no operation moved by 1% of the time
where the time goes in v6:
time: 26.9 us; the launch traced here: 26.8 us
  Pallas kernels  26.1 us (97%)
  between operations  0.64 us (2%)
    pallas_call x1, Pallas kernels, body(): pl.pallas_call(functools.partial(kernel, spaces, beads), out_shape=(moved...  25.4 us
    pallas_call x1, Pallas kernels, body(): pl.pallas_call(put_out, out_shape=(plain, plain), in_specs=[anywhere] * 2...  0.76 us

profile of v6, /device:TPU:8, one launch (start us, length us, event | category | flops | bytes accessed | tf_op | source)
XLA Modules:
  0.0 26.8 jit_solution(7091841978653612493)
XLA Ops:
  0.6 25.4 %shard_map.95 = (f32[3,4,4096]{2,1,0:T(4,128)S(1)}, f32[3,4,4096]{2,1,0:T(4,128)S(1)}) custom-call(f32[3,4,4096]{2,1,0:T(4,128)} %bitcast.6, f32[3,4,4096]{2,1,0:T(4,128)} %bitcast.7, f32[32,128]{1,0:T(8,128)} %bitcast.8, f32[32,128]{1,0:T(8,128)} %bitcast.9, s32[2,4096]{1,0:T(2,128)} %bond_in.1, s32[3,2048]{1,0:T(4,128)} %angle_in.1, s32[3,32]{1,0:T(4,128)} %nbr_in.1, ...), custom_call_target="tpu_custom_call" | custom-call | tf_op jit(solution)/shard_map/pallas_call | solution.py:555
  26.0 0.8 %shard_map.96 = (f32[3,4,4096]{2,1,0:T(4,128)}, f32[3,4,4096]{2,1,0:T(4,128)}) custom-call(f32[3,4,4096]{2,1,0:T(4,128)S(1)} %get-tuple-element.6.q_ref, f32[3,4,4096]{2,1,0:T(4,128)S(1)} %get-tuple-element.7.p_ref), custom_call_target="tpu_custom_call" | custom-call | tf_op jit(solution)/shard_map/pallas_call | solution.py:599

commit v7 on v6

--- a/solution.py
+++ b/solution.py
@@ -26,7 +26,6 @@
 angle_stiff = 0.1
 angle_rest = 0.5
 range_sq = 4.0
-CHUNK = 2
 
 F32 = jnp.float32
 BF16 = jnp.bfloat16
@@ -377,7 +376,7 @@
         for u in list(range(GT)) + list(range(GT + tiles, 2 * GT + tiles)):
             sides(turn, u, False)
 
-    def nonbonded(turn, finish, chunk):
+    def nonbonded(turn, finish, ends):
         base = spot * tiles - GT
         count = total * tiles
         found = []
@@ -401,7 +400,7 @@
                 both = lanes(got, k)
                 force = jnp.where((row16 >= 3 * k) & (row16 < 3 * k + 3), rows * both[12:13] - both, force)
             found.append(force * strengths[t])
-            if len(found) == chunk:
+            if t + 1 in ends:
                 finish(t, jnp.concatenate(found, axis=1))
                 found = []
 
@@ -474,7 +473,7 @@
         found.append(force)
 
     prepare(0)
-    nonbonded(0, keep, tiles)
+    nonbonded(0, keep, (tiles,))
     high, low = split2(found[0] * inverse)
     shift = mm(kick_table, jnp.concatenate([high, high, low], axis=0))
     current = [x + shift[2 * BEADS * c : 2 * BEADS * c + BEADS] for c, x in enumerate(current)]
@@ -496,8 +495,8 @@
     def send_home(t, force):
         high, low = split2(force)
         kick = mm(wide_table, jnp.concatenate([high, high, low], axis=0))
-        width = CHUNK * TILE
-        begin = (t + 1 - CHUNK) * TILE
+        width = force.shape[1]
+        begin = (t + 1) * TILE - width
         for c in range(3):
             p_done[c, :, begin : begin + width] = (
                 moment[c][:, begin : begin + width] + kick[c * BEADS : (c + 1) * BEADS]
@@ -514,12 +513,12 @@
                 device_id=(space, peers[n]),
                 device_id_type=MESH,
             ).start()
-        mine = pltpu.make_async_copy(p_done.at[:, my_rows, begin : begin + width], target, own_sem.at[1 + t // CHUNK])
+        mine = pltpu.make_async_copy(p_done.at[:, my_rows, begin : begin + width], target, own_sem.at[t + 3 - tiles])
         mine.start()
         late.append(mine)
 
     prepare(1)
-    nonbonded(1, send_home, CHUNK)
+    nonbonded(1, send_home, (tiles - 1, tiles))
     for kind in range(4):
         wait_all(send_sem.at[kind])
     for turn in range(2):
@@ -579,7 +578,7 @@
                 pltpu.SemaphoreType.DMA((10,)),
                 pltpu.SemaphoreType.DMA((4,)),
                 pltpu.SemaphoreType.DMA((4,)),
-                pltpu.SemaphoreType.DMA((1 + tiles // CHUNK,)),
+                pltpu.SemaphoreType.DMA((3,)),
                 pltpu.SemaphoreType.DMA((2,)),
                 pltpu.SemaphoreType.DMA((2,)),
             ],

time: 26.9 us -> 26.9 us (level)
  no operation moved by 1% of the time
where the time goes in v7:
time: 26.9 us; the launch traced here: 26.8 us
  Pallas kernels  26.1 us (97%)
  between operations  0.64 us (2%)
    pallas_call x1, Pallas kernels, body(): pl.pallas_call(functools.partial(kernel, spaces, beads), out_shape=(moved...  25.4 us
    pallas_call x1, Pallas kernels, body(): pl.pallas_call(put_out, out_shape=(plain, plain), in_specs=[anywhere] * 2...  0.76 us

profile of v7, /device:TPU:8, one launch (start us, length us, event | category | flops | bytes accessed | tf_op | source)
XLA Modules:
  0.0 26.8 jit_solution(16742214598114522545)
XLA Ops:
  0.6 25.4 %shard_map.95 = (f32[3,4,4096]{2,1,0:T(4,128)S(1)}, f32[3,4,4096]{2,1,0:T(4,128)S(1)}) custom-call(f32[3,4,4096]{2,1,0:T(4,128)} %bitcast.6, f32[3,4,4096]{2,1,0:T(4,128)} %bitcast.7, f32[32,128]{1,0:T(8,128)} %bitcast.8, f32[32,128]{1,0:T(8,128)} %bitcast.9, s32[2,4096]{1,0:T(2,128)} %bond_in.1, s32[3,2048]{1,0:T(4,128)} %angle_in.1, s32[3,32]{1,0:T(4,128)} %nbr_in.1, ...), custom_call_target="tpu_custom_call" | custom-call | tf_op jit(solution)/shard_map/pallas_call | solution.py:554
  26.0 0.8 %shard_map.96 = (f32[3,4,4096]{2,1,0:T(4,128)}, f32[3,4,4096]{2,1,0:T(4,128)}) custom-call(f32[3,4,4096]{2,1,0:T(4,128)S(1)} %get-tuple-element.6.q_ref, f32[3,4,4096]{2,1,0:T(4,128)S(1)} %get-tuple-element.7.p_ref), custom_call_target="tpu_custom_call" | custom-call | tf_op jit(solution)/shard_map/pallas_call | solution.py:598
